TPU v7x, 32 devices: a whole 2x2x4 slice. The times are simulated.
32 devices in a mesh: fsdp: 4 (over x, core), ep: 8 (over z, y).
Axes of the slice: x: 2, y: 2, z: 4, core: 2. Of those that a mesh axis runs over, the one named last changes fastest.
Arguments:
- tokens: bfloat16 [256, 2048], P(('fsdp', 'ep')), may hold values from -6 to 6
- cotangent: bfloat16 [256, 2048], P(('fsdp', 'ep')), may hold values from -4 to 4
- routes: int32 [256, 2], P(('fsdp', 'ep')), may hold values from 0 to 7, as said below
- logits: float32 [256, 8], P(('fsdp', 'ep')), may hold values from -8 to 8
- w_gate: bfloat16 [2048, 16384], P('fsdp', 'ep'), may hold values from -0.125 to 0.125
- w_up: bfloat16 [2048, 16384], P('fsdp', 'ep'), may hold values from -0.125 to 0.125
- w_down: bfloat16 [16384, 2048], P('ep', 'fsdp'), may hold values from -0.0625 to 0.0625
Outputs:
- grad_tokens: bfloat16 [256, 2048], P(('fsdp', 'ep'))
- route_dot: float32 [256, 2], P(('fsdp', 'ep'))
- aux_grad: float32 [256, 8], P(('fsdp', 'ep'))
- grad_gate: bfloat16 [2048, 16384], P('fsdp', 'ep')
- grad_up: bfloat16 [2048, 16384], P('fsdp', 'ep')
- grad_down: bfloat16 [16384, 2048], P('ep', 'fsdp')
Inputs may be any that keep to these rules, and one draw needn't show every extreme that they name: `routes`: each token names two different experts; on every device at most 3 tokens name one expert, and some expert is named by exactly 3 of them.
All inputs are finite; a program needn't handle non-finite values.
Results may differ from a plain program's by a relative error of at most 0.04.
Values may be sent and summed in bfloat16 or wider, within the bound.
A program may use at most 128 MiB of HBM per device.

v0:
```python
import functools

import jax
import jax.numpy as jnp
from jax import lax
from jax.experimental import pallas as pl
from jax.experimental.pallas import tpu as pltpu
from jax.sharding import PartitionSpec as P

EXP_WIN = 2
CAP = 3
PAD = 8
CORES = 2
CHUNKS = 4
GROUPS = 2
LAST = (((1,), (1,)), ((), ()))
FIRST = (((0,), (0,)), ((), ()))
F32 = jnp.float32
BF16 = jnp.bfloat16
MESH = pl.DeviceIdType.MESH


def iota(shape, axis):
    return lax.broadcasted_iota(jnp.int32, shape, axis)


def kernel(
    n_fsdp, n_ep, chunks,
    tok_ref, cot_ref, routes_ref, logits_ref, wg_hbm, wu_hbm, wd_hbm,
    gt_ref, rd_ref, aux_ref, x_hbm, dy_hbm, acts_hbm,
    wg, wu, wd,
    send1, recv1, rows_x, rows_dy,
    own_a, send_a, recv_a, send_b, recv_b, acts, recv_c, dx, dots, send2, recv2,
    w_sem, o_sem, x_sem, d_send, d_recv, a_send, a_recv, b_send, b_recv, c_send, c_recv, r_send, r_recv,
):
    n_dev = n_fsdp * n_ep
    n_x = n_fsdp // CORES
    blocks = n_ep // EXP_WIN
    f, e = lax.axis_index("fsdp"), lax.axis_index("ep")
    me = f * n_ep + e
    x, core = f // CORES, lax.rem(f, CORES)
    partner = x * CORES + (1 - core)
    depth, width = wg.shape
    half = width // CORES
    w = half // chunks
    ring = n_ep // GROUPS
    size = n_fsdp * ring
    span_rows = size * CAP
    place = f * ring + e // GROUPS

    def peer(t, i):
        return i // ring, lax.rem(i, ring) * GROUPS + lax.rem(e + t, GROUPS)

    barrier = pltpu.get_barrier_semaphore()

    def greet(j, _):
        d = lax.rem(me + j, n_dev)
        pl.semaphore_signal(barrier, inc=1, device_id=(d // n_ep, lax.rem(d, n_ep)), device_id_type=MESH)
        return 0

    lax.fori_loop(1, n_dev, greet, 0)
    loads = [
        pltpu.make_async_copy(s, t, w_sem.at[i])
        for i, (s, t) in enumerate(((wg_hbm, wg), (wu_hbm, wu), (wd_hbm, wd)))
    ]
    for c in loads:
        c.start()

    routes = routes_ref[...]
    logits = logits_ref[...]
    n_tok, n_exp = logits.shape
    ti, tj = iota((n_tok, n_tok), 0), iota((n_tok, n_tok), 1)
    r0, r1 = (
        jnp.sum(jnp.where(ti == tj, routes[k : k + 1, :], 0), axis=1, keepdims=True) for k in range(2)
    )
    experts = iota((n_tok, n_exp), 1)
    c0 = jnp.sum(jnp.where(experts == r0, logits, 0.0), axis=1, keepdims=True)
    c1 = jnp.sum(jnp.where(experts == r1, logits, 0.0), axis=1, keepdims=True)
    top = jnp.maximum(c0, c1)
    e0, e1 = jnp.exp(c0 - top), jnp.exp(c1 - top)
    p0, p1 = e0 / (e0 + e1), e1 / (e0 + e1)
    ci = iota((PAD, n_tok), 0)
    lanes = iota((n_tok, depth), 1)
    counts = jnp.sum(
        jnp.where(lanes == r0, 1.0, 0.0) + jnp.where(lanes == r1, 1.0, 0.0), axis=0, keepdims=True
    )
    tok = tok_ref[...]
    cot = cot_ref[...].astype(F32)
    member_col, slot_col, member_row, slot_line = [], [], [], []
    row_id = iota((PAD, depth), 0)
    for k in range(EXP_WIN):
        m0, m1 = jnp.where(r0 == k, 1.0, 0.0), jnp.where(r1 == k, 1.0, 0.0)
        col = m0 + m1
        weight = m0 * p0 + m1 * p1
        row = jnp.sum(jnp.where(ti == tj, col, 0.0), axis=0, keepdims=True)
        slot_row = jnp.sum(jnp.where(ti < tj, col, 0.0), axis=0, keepdims=True)
        slot_col.append(jnp.sum(jnp.where(tj < ti, row, 0.0), axis=1, keepdims=True))
        member_col.append(col)
        member_row.append(row)
        slot_line.append(slot_row)
        cf = ci.astype(F32)
        sel_a = jnp.where((cf == slot_row) & (ci < CAP), row, 0.0).astype(BF16)
        sel_b = jnp.where((cf - CAP == slot_row) & (ci < 2 * CAP), row, 0.0).astype(BF16)
        wcot = (cot * weight).astype(BF16)
        sent = jnp.dot(sel_a, tok, preferred_element_type=F32)
        sent = sent + jnp.dot(sel_b, wcot, preferred_element_type=F32)
        for g in range(n_fsdp):
            part = sent[:, g * depth : (g + 1) * depth]
            send1[k, g] = jnp.where(row_id == 2 * CAP, counts, part).astype(BF16)

    pl.semaphore_wait(barrier, n_dev - 1)

    recv1[place] = send1[e // blocks, f]
    for t in range(GROUPS):
        back_t = (GROUPS - t) % GROUPS

        def push(j, _, t=t, back_t=back_t):
            df, de = peer(t, lax.rem(place + j, size))
            pltpu.make_async_remote_copy(
                src_ref=send1.at[de // blocks, df], dst_ref=recv1.at[back_t * size + place],
                send_sem=d_send, recv_sem=d_recv.at[back_t], device_id=(df, de), device_id_type=MESH,
            ).start()
            return 0

        lax.fori_loop(1 if t == 0 else 0, size, push, 0)

    grp = min(16, size)
    si, sj = iota((grp * CAP, grp * PAD), 0), iota((grp * CAP, grp * PAD), 1)
    base = (si // CAP) * PAD + lax.rem(si, CAP)
    pick_x = jnp.where(sj == base, 1.0, 0.0).astype(BF16)
    pick_dy = jnp.where(sj == base + CAP, 1.0, 0.0).astype(BF16)
    pick_c = jnp.where(
        lax.rem(iota((8, grp * PAD), 1), PAD) == 2 * CAP, 1.0, 0.0
    ).astype(BF16)

    def prepare(t, total):
        landed = recv1.at[pl.ds(t * size, size - 1 if t == 0 else size)]
        pltpu.make_async_copy(landed, landed, d_recv.at[t]).wait()
        for g in range(t * size // grp, (t + 1) * size // grp):
            came = recv1[g * grp : (g + 1) * grp].reshape(grp * PAD, depth)
            span = pl.ds(g * grp * CAP, grp * CAP)
            rows_x[span] = jnp.dot(pick_x, came, preferred_element_type=F32).astype(BF16)
            rows_dy[span] = jnp.dot(pick_dy, came, preferred_element_type=F32).astype(BF16)
            total = total + jnp.dot(pick_c, came, preferred_element_type=F32)
        return total

    def copy_a(k):
        return pltpu.make_async_remote_copy(
            src_ref=send_a.at[k], dst_ref=recv_a.at[k], send_sem=a_send.at[k], recv_sem=a_recv.at[k],
            device_id=(partner, e), device_id_type=MESH,
        )

    def copy_b(k, j):
        to = lax.rem(x + j, n_x) * CORES + core
        return pltpu.make_async_remote_copy(
            src_ref=send_b.at[k], dst_ref=recv_b.at[k, j - 1], send_sem=b_send.at[k, j - 1],
            recv_sem=b_recv.at[k, j - 1], device_id=(to, e), device_id_type=MESH,
        )

    def copy_c(k):
        return pltpu.make_async_remote_copy(
            src_ref=acts.at[k], dst_ref=recv_c.at[k], send_sem=c_send.at[k], recv_sem=c_recv.at[k],
            device_id=(partner, e), device_id_type=MESH,
        )

    def columns(h, k):
        return pl.ds(pl.multiple_of(h * half + k * w, w), w)

    def group(u):
        return pl.ds(u // chunks * span_rows, span_rows)

    def partials(h, u):
        cols = columns(h, u % chunks)
        xs, dys = rows_x[group(u)], rows_dy[group(u)]
        yield jnp.dot(xs, wg[:, cols], preferred_element_type=F32)
        yield jnp.dot(xs, wu[:, cols], preferred_element_type=F32)
        yield lax.dot_general(dys, wd[cols, :], LAST, preferred_element_type=F32)

    def stage1(k):
        for i, v in enumerate(partials(1 - core, k)):
            send_a[k, i] = v.astype(BF16)
        copy_a(k).start()
        for i, v in enumerate(partials(core, k)):
            own_a[k, i] = v

    def stage2(k):
        copy_a(k).wait_recv()
        v = own_a[k] + recv_a[k].astype(F32)
        own_a[k] = v
        send_b[k] = v.astype(BF16)
        for j in range(1, n_x):
            copy_b(k, j).start()

    def stage3(k):
        for j in range(1, n_x):
            copy_b(k, j).wait_recv()
        pre = []
        for i in range(3):
            v = own_a[k, i]
            for j in range(n_x - 1):
                v = v + recv_b[k, j, i].astype(F32)
            pre.append(v)
        gate_pre, up_pre, hidden_grad = pre
        sigma = jax.nn.sigmoid(gate_pre)
        active = gate_pre * sigma
        hidden = (active * up_pre).astype(BF16)
        dot = jnp.sum(hidden.astype(F32) * hidden_grad, axis=1, keepdims=True)
        dots[group(k)] = dot if k % chunks == 0 else dots[group(k)] + dot
        acts[k, 0] = (hidden_grad * up_pre * sigma * (1.0 + gate_pre * (1.0 - sigma))).astype(BF16)
        acts[k, 1] = (hidden_grad * active).astype(BF16)
        acts[k, 2] = hidden
        copy_c(k).start()

    def grads(h, k, source):
        cols = columns(h, k % chunks)
        part = lax.dot_general(source[k, 0], wg[:, cols], LAST, preferred_element_type=F32)
        return part + lax.dot_general(source[k, 1], wu[:, cols], LAST, preferred_element_type=F32)

    def store(h, k, slot, source):
        return pltpu.make_async_copy(source.at[k], acts_hbm.at[h, k % chunks, :, group(k), :], o_sem.at[k, slot])

    row_stores = [
        pltpu.make_async_copy(rows_x, x_hbm, x_sem.at[0]),
        pltpu.make_async_copy(rows_dy, dy_hbm, x_sem.at[1]),
    ]

    def stage4(k):
        part = grads(core, k, acts)
        store(core, k, 0, acts).start()
        copy_c(k).wait_recv()
        part = part + grads(1 - core, k, recv_c)
        store(1 - core, k, 1, recv_c).start()
        dx[group(k)] = part if k % chunks == 0 else dx[group(k)] + part

    for c in loads:
        c.wait()
    total = jnp.zeros((8, depth), F32)
    for t in range(GROUPS):
        total = prepare(t, total)
        for k in range(t * chunks, (t + 1) * chunks):
            stage1(k)
            if k > 0:
                stage2(k - 1)
    stage2(GROUPS * chunks - 1)

    for c in row_stores:
        c.start()

    count = total[0:1, 0:n_exp]
    target = n_exp * (count / jnp.sum(count, axis=1, keepdims=True))
    raised = jnp.exp(logits - jnp.max(logits, axis=1, keepdims=True))
    probs = raised / jnp.sum(raised, axis=1, keepdims=True)
    aux_ref[...] = probs * (target - jnp.sum(probs * target, axis=1, keepdims=True))

    bi, bj = iota((grp * PAD, grp * CAP), 0), iota((grp * PAD, grp * CAP), 1)
    base = (bj // CAP) * PAD + lax.rem(bj, CAP)
    put_x = jnp.where(bi == base, 1.0, 0.0).astype(BF16)
    put_dot = jnp.where(bi == base + CAP, 1.0, 0.0).astype(BF16)
    once = jnp.where(x == 0, 1.0, 0.0)

    def give_back(t):
        for g in range(t * size // grp, (t + 1) * size // grp):
            span = pl.ds(g * grp * CAP, grp * CAP)
            mine = jnp.broadcast_to(dots[span] * once, (grp * CAP, depth)).astype(BF16)
            back = jnp.dot(put_x, dx[span].astype(BF16), preferred_element_type=F32)
            back = back + jnp.dot(put_dot, mine, preferred_element_type=F32)
            send2[g * grp : (g + 1) * grp] = back.astype(BF16).reshape(grp, PAD, depth)

        def give(j, _):
            i = lax.rem(place + j, size)
            pltpu.make_async_remote_copy(
                src_ref=send2.at[t * size + i], dst_ref=recv2.at[me], send_sem=r_send, recv_sem=r_recv,
                device_id=peer(t, i), device_id_type=MESH,
            ).start()
            return 0

        lax.fori_loop(1 if t == 0 else 0, size, give, 0)
        if t == 0:
            recv2[me] = send2[place]

    for k in range(GROUPS * chunks):
        stage3(k)
        if k > 0:
            stage4(k - 1)
            if k % chunks == 0:
                give_back(k // chunks - 1)
    stage4(GROUPS * chunks - 1)
    give_back(GROUPS - 1)
    everyone = recv1.at[pl.ds(0, n_dev - 1)]
    everyone2 = recv2.at[pl.ds(0, n_dev - 1)]
    pltpu.make_async_copy(everyone2, everyone2, r_recv).wait()

    route = [jnp.zeros((1, 1), F32) for _ in range(EXP_WIN * CAP)]
    for g in range(n_fsdp):
        grad = jnp.zeros((n_tok, depth), F32)
        for k in range(EXP_WIN):
            acc = recv2[g * n_ep + k * blocks].astype(F32)
            for b in range(1, blocks):
                acc = acc + recv2[g * n_ep + k * blocks + b].astype(F32)
            for c in range(CAP):
                pick = jnp.where(slot_col[k] == c, member_col[k], 0.0)
                grad = grad + pick * acc[c : c + 1, :]
                route[k * CAP + c] = route[k * CAP + c] + acc[CAP + c : CAP + c + 1, 0:1]
        gt_ref[:, g * depth : (g + 1) * depth] = grad.astype(BF16)
    which = iota((EXP_WIN, n_tok), 0)
    out = jnp.zeros((EXP_WIN, n_tok), F32)
    for k in range(EXP_WIN):
        for c in range(CAP):
            pick = jnp.where(slot_line[k] == c, member_row[k], 0.0)
            out = out + jnp.where(which == k, pick * route[k * CAP + c], 0.0)
    rd_ref[...] = out

    pltpu.make_async_copy(everyone, everyone, d_send).wait()
    pltpu.make_async_copy(everyone2, everyone2, r_send).wait()
    for k in range(GROUPS * chunks):
        copy_a(k).wait_send()
        copy_c(k).wait_send()
        for j in range(1, n_x):
            copy_b(k, j).wait_send()
        store(core, k, 0, acts).wait()
        store(1 - core, k, 1, recv_c).wait()
    for c in row_stores:
        c.wait()


def weight_kernel(x_ref, dy_ref, acts_ref, gt_in, rd_in, aux_in, gt_ref, rd_ref, aux_ref, og, ou, od):
    xs, dys = x_ref[...], dy_ref[...]
    for p in range(acts_ref.shape[0]):
        w = acts_ref.shape[3]
        c = pl.ds(p * w, w)
        og[:, c] = lax.dot_general(xs, acts_ref[p, 0], FIRST, preferred_element_type=F32).astype(BF16)
        ou[:, c] = lax.dot_general(xs, acts_ref[p, 1], FIRST, preferred_element_type=F32).astype(BF16)
        od[c, :] = lax.dot_general(acts_ref[p, 2], dys, FIRST, preferred_element_type=F32).astype(BF16)

    @pl.when(pl.program_id(0) == 0)
    def _():
        gt_ref[...] = gt_in[...]
        rd_ref[...] = rd_in[...]
        aux_ref[...] = aux_in[...]


def body(n_fsdp, n_ep, tokens, cotangent, routes, logits, w_gate, w_up, w_down):
    n_tok, model = tokens.shape
    depth, width = w_gate.shape
    n_dev = n_fsdp * n_ep
    n_x = n_fsdp // CORES
    rows = n_dev * CAP
    half = width // CORES
    chunks = max(1, min(CHUNKS, half // 128))
    w = half // chunks
    items, part = GROUPS * chunks, rows // GROUPS
    vmem = pl.BlockSpec(memory_space=pltpu.VMEM)
    hbm = pl.BlockSpec(memory_space=pl.ANY)
    dma = pltpu.SemaphoreType.DMA
    small_x, small_r, small_a, all_x, all_dy, all_acts = pl.pallas_call(
        functools.partial(kernel, n_fsdp, n_ep, chunks),
        out_shape=(
            jax.ShapeDtypeStruct((n_tok, model), BF16),
            jax.ShapeDtypeStruct((EXP_WIN, n_tok), F32),
            jax.ShapeDtypeStruct(logits.shape, F32),
            jax.ShapeDtypeStruct((rows, depth), BF16),
            jax.ShapeDtypeStruct((rows, depth), BF16),
            jax.ShapeDtypeStruct((CORES, chunks, 3, rows, w), BF16),
        ),
        in_specs=[vmem] * 4 + [hbm] * 3,
        out_specs=[vmem] * 3 + [hbm] * 3,
        scratch_shapes=[
            pltpu.VMEM(w_gate.shape, BF16),
            pltpu.VMEM(w_up.shape, BF16),
            pltpu.VMEM(w_down.shape, BF16),
            pltpu.VMEM((EXP_WIN, n_fsdp, PAD, depth), BF16),
            pltpu.VMEM((n_dev, PAD, depth), BF16),
            pltpu.VMEM((rows, depth), BF16),
            pltpu.VMEM((rows, depth), BF16),
            pltpu.VMEM((items, 3, part, w), F32),
            pltpu.VMEM((items, 3, part, w), BF16),
            pltpu.VMEM((items, 3, part, w), BF16),
            pltpu.VMEM((items, 3, part, w), BF16),
            pltpu.VMEM((items, n_x - 1, 3, part, w), BF16),
            pltpu.VMEM((items, 3, part, w), BF16),
            pltpu.VMEM((items, 3, part, w), BF16),
            pltpu.VMEM((rows, depth), F32),
            pltpu.VMEM((rows, 1), F32),
            pltpu.VMEM((n_dev, PAD, depth), BF16),
            pltpu.VMEM((n_dev, PAD, depth), BF16),
            dma((3,)),
            dma((items, CORES)),
            dma((2,)),
            dma,
            dma((GROUPS,)),
            dma((items,)),
            dma((items,)),
            dma((items, n_x - 1)),
            dma((items, n_x - 1)),
            dma((items,)),
            dma((items,)),
            dma,
            dma,
        ],
        compiler_params=pltpu.CompilerParams(
            collective_id=0, has_side_effects=True, vmem_limit_bytes=62 * 1024 * 1024
        ),
    )(tokens, cotangent, jnp.transpose(routes), logits, w_gate, w_up, w_down)
    pair = 2 if chunks % 2 == 0 else 1
    step = w * pair
    per = chunks // pair

    def same(i):
        return (0, 0)

    def whole(a):
        return pl.BlockSpec(a.shape, same)

    smalls = [whole(small_x), whole(small_r), whole(small_a)]
    cols = pl.BlockSpec((depth, step), lambda i: (0, i))
    out = pl.pallas_call(
        weight_kernel,
        grid=(width // step,),
        out_shape=(
            jax.ShapeDtypeStruct(small_x.shape, BF16),
            jax.ShapeDtypeStruct(small_r.shape, F32),
            jax.ShapeDtypeStruct(small_a.shape, F32),
            jax.ShapeDtypeStruct(w_gate.shape, BF16),
            jax.ShapeDtypeStruct(w_up.shape, BF16),
            jax.ShapeDtypeStruct(w_down.shape, BF16),
        ),
        in_specs=[
            whole(all_x),
            whole(all_dy),
            pl.BlockSpec(
                (None, pair, 3, rows, w),
                lambda i: (i // per, lax.rem(i, per), 0, 0, 0),
            ),
        ]
        + smalls,
        out_specs=smalls + [cols, cols, pl.BlockSpec((step, depth), lambda i: (i, 0))],
        compiler_params=pltpu.CompilerParams(dimension_semantics=("arbitrary",)),
    )(all_x, all_dy, all_acts, small_x, small_r, small_a)
    return (out[0], jnp.transpose(out[1])) + tuple(out[2:])


def solution(mesh):
    in_specs = (
        P(("fsdp", "ep"), None),
        P(("fsdp", "ep"), None),
        P(("fsdp", "ep"), None),
        P(("fsdp", "ep"), None),
        P("fsdp", "ep"),
        P("fsdp", "ep"),
        P("ep", "fsdp"),
    )
    out_specs = (
        P(("fsdp", "ep"), None),
        P(("fsdp", "ep"), None),
        P(("fsdp", "ep"), None),
        P("fsdp", "ep"),
        P("fsdp", "ep"),
        P("ep", "fsdp"),
    )
    step = functools.partial(body, mesh.shape["fsdp"], mesh.shape["ep"])
    return jax.shard_map(step, mesh=mesh, in_specs=in_specs, out_specs=out_specs, check_vma=False)
```

profile of v0, /device:TPU:0, one launch (start us, length us, event | category | flops | bytes accessed | tf_op | source)
XLA Modules:
  0.0 45.3 jit_solution(3300402436075984129)
XLA Ops:
  0.6 39.0 %shard_map.118 = (bf16[8,2048]{1,0:T(8,128)(2,1)}, f32[2,8]{1,0:T(2,128)}, f32[8,8]{1,0:T(8,128)}, bf16[96,512]{1,0:T(8,128)(2,1)}, bf16[96,512]{1,0:T(8,128)(2,1)}, /*index=5*/bf16[2,4,3,96,256]{4,3,2,1,0:T(8,128)(2,1)}) custom-call(bf16[8,2048]{1,0:T(8,128)(2,1)} %tok_ref.1, bf16[8,2048]{1,0:T(8,128)(2,1)} %cot_ref.1, s32[2,8]{1,0:T(2,128)} %bitcast.2, ...), custom_call_target="tpu_custom_call" | custom-call | tf_op jit(solution)/shard_map/pallas_call | solution.py:355
  39.7 5.6 %shard_map.119 = (bf16[8,2048]{1,0:T(8,128)(2,1)}, f32[2,8]{1,0:T(2,128)}, f32[8,8]{1,0:T(8,128)}, bf16[512,2048]{1,0:T(8,128)(2,1)}, bf16[512,2048]{1,0:T(8,128)(2,1)}, /*index=5*/bf16[2048,512]{1,0:T(8,128)(2,1)}) custom-call(bf16[96,512]{1,0:T(8,128)(2,1)} %get-tuple-element.18.x_ref, bf16[96,512]{1,0:T(8,128)(2,1)} %get-tuple-element.19.dy_ref, ...), custom_call_target="tpu_custom_call" | custom-call | tf_op jit(solution)/shard_map/pallas_call | solution.py:416
where the time goes:
time: 45.5 us; the launch traced here: 45.3 us
  Pallas kernels  44.6 us (98%)
  between operations  0.64 us (1%)
    pallas_call x1, Pallas kernels, body(): pl.pallas_call(functools.partial(kernel, n_fsdp, n_ep, chunks), out_shape...  39 us
    pallas_call x1, Pallas kernels, body(): pl.pallas_call(weight_kernel, grid=(width // step,), out_shape=(jax.Shape...  5.61 us

commit v1 on v0

--- a/solution.py
+++ b/solution.py
@@ -13,6 +13,7 @@
 CORES = 2
 CHUNKS = 4
 GROUPS = 2
+PIECES = 4
 LAST = (((1,), (1,)), ((), ()))
 FIRST = (((0,), (0,)), ((), ()))
 F32 = jnp.float32
@@ -27,11 +28,11 @@
 def kernel(
     n_fsdp, n_ep, chunks,
     tok_ref, cot_ref, routes_ref, logits_ref, wg_hbm, wu_hbm, wd_hbm,
-    gt_ref, rd_ref, aux_ref, x_hbm, dy_hbm, acts_hbm,
+    gt_ref, rd_ref, aux_ref, og, ou, od,
     wg, wu, wd,
     send1, recv1, rows_x, rows_dy,
     own_a, send_a, recv_a, send_b, recv_b, acts, recv_c, dx, dots, send2, recv2,
-    w_sem, o_sem, x_sem, d_send, d_recv, a_send, a_recv, b_send, b_recv, c_send, c_recv, r_send, r_recv,
+    w_sem, d_send, d_recv, a_send, a_recv, b_send, b_recv, c_send, c_recv, r_send, r_recv,
 ):
     n_dev = n_fsdp * n_ep
     n_x = n_fsdp // CORES
@@ -216,20 +217,21 @@
         part = lax.dot_general(source[k, 0], wg[:, cols], LAST, preferred_element_type=F32)
         return part + lax.dot_general(source[k, 1], wu[:, cols], LAST, preferred_element_type=F32)
 
-    def store(h, k, slot, source):
-        return pltpu.make_async_copy(source.at[k], acts_hbm.at[h, k % chunks, :, group(k), :], o_sem.at[k, slot])
-
-    row_stores = [
-        pltpu.make_async_copy(rows_x, x_hbm, x_sem.at[0]),
-        pltpu.make_async_copy(rows_dy, dy_hbm, x_sem.at[1]),
-    ]
+    def weights(c):
+        for h, source in ((core, acts), (1 - core, recv_c)):
+            cols = columns(h, c)
+            ga, ua, hid = (
+                jnp.concatenate([source[t * chunks + c, i] for t in range(GROUPS)], axis=0) for i in range(3)
+            )
+            xs, dys = rows_x[...], rows_dy[...]
+            og[:, cols] = lax.dot_general(xs, ga, FIRST, preferred_element_type=F32).astype(BF16)
+            ou[:, cols] = lax.dot_general(xs, ua, FIRST, preferred_element_type=F32).astype(BF16)
+            od[cols, :] = lax.dot_general(hid, dys, FIRST, preferred_element_type=F32).astype(BF16)
 
     def stage4(k):
         part = grads(core, k, acts)
-        store(core, k, 0, acts).start()
         copy_c(k).wait_recv()
         part = part + grads(1 - core, k, recv_c)
-        store(1 - core, k, 1, recv_c).start()
         dx[group(k)] = part if k % chunks == 0 else dx[group(k)] + part
 
     for c in loads:
@@ -243,9 +245,6 @@
                 stage2(k - 1)
     stage2(GROUPS * chunks - 1)
 
-    for c in row_stores:
-        c.start()
-
     count = total[0:1, 0:n_exp]
     target = n_exp * (count / jnp.sum(count, axis=1, keepdims=True))
     raised = jnp.exp(logits - jnp.max(logits, axis=1, keepdims=True))
@@ -286,6 +285,8 @@
                 give_back(k // chunks - 1)
     stage4(GROUPS * chunks - 1)
     give_back(GROUPS - 1)
+    for c in range(chunks):
+        weights(c)
     everyone = recv1.at[pl.ds(0, n_dev - 1)]
     everyone2 = recv2.at[pl.ds(0, n_dev - 1)]
     pltpu.make_async_copy(everyone2, everyone2, r_recv).wait()
@@ -317,26 +318,21 @@
         copy_c(k).wait_send()
         for j in range(1, n_x):
             copy_b(k, j).wait_send()
-        store(core, k, 0, acts).wait()
-        store(1 - core, k, 1, recv_c).wait()
-    for c in row_stores:
+
+
+def put_kernel(n, *refs):
+    sources, targets, sem = refs[:n], refs[n : 2 * n], refs[2 * n]
+    copies = []
+    for s, t in zip(sources, targets):
+        rows = s.shape[0]
+        pieces = PIECES if rows % (16 * PIECES) == 0 else 1
+        for p in range(pieces):
+            span = pl.ds(p * (rows // pieces), rows // pieces)
+            copies.append(pltpu.make_async_copy(s.at[span], t.at[span], sem.at[len(copies)]))
+    for c in copies:
+        c.start()
+    for c in copies:
         c.wait()
-
-
-def weight_kernel(x_ref, dy_ref, acts_ref, gt_in, rd_in, aux_in, gt_ref, rd_ref, aux_ref, og, ou, od):
-    xs, dys = x_ref[...], dy_ref[...]
-    for p in range(acts_ref.shape[0]):
-        w = acts_ref.shape[3]
-        c = pl.ds(p * w, w)
-        og[:, c] = lax.dot_general(xs, acts_ref[p, 0], FIRST, preferred_element_type=F32).astype(BF16)
-        ou[:, c] = lax.dot_general(xs, acts_ref[p, 1], FIRST, preferred_element_type=F32).astype(BF16)
-        od[c, :] = lax.dot_general(acts_ref[p, 2], dys, FIRST, preferred_element_type=F32).astype(BF16)
-
-    @pl.when(pl.program_id(0) == 0)
-    def _():
-        gt_ref[...] = gt_in[...]
-        rd_ref[...] = rd_in[...]
-        aux_ref[...] = aux_in[...]
 
 
 def body(n_fsdp, n_ep, tokens, cotangent, routes, logits, w_gate, w_up, w_down):
@@ -352,18 +348,19 @@
     vmem = pl.BlockSpec(memory_space=pltpu.VMEM)
     hbm = pl.BlockSpec(memory_space=pl.ANY)
     dma = pltpu.SemaphoreType.DMA
-    small_x, small_r, small_a, all_x, all_dy, all_acts = pl.pallas_call(
+    made = (
+        ((n_tok, model), BF16),
+        ((EXP_WIN, n_tok), F32),
+        (logits.shape, F32),
+        (w_gate.shape, BF16),
+        (w_up.shape, BF16),
+        (w_down.shape, BF16),
+    )
+    held = pl.pallas_call(
         functools.partial(kernel, n_fsdp, n_ep, chunks),
-        out_shape=(
-            jax.ShapeDtypeStruct((n_tok, model), BF16),
-            jax.ShapeDtypeStruct((EXP_WIN, n_tok), F32),
-            jax.ShapeDtypeStruct(logits.shape, F32),
-            jax.ShapeDtypeStruct((rows, depth), BF16),
-            jax.ShapeDtypeStruct((rows, depth), BF16),
-            jax.ShapeDtypeStruct((CORES, chunks, 3, rows, w), BF16),
-        ),
+        out_shape=tuple(pltpu.VMEM(d, t) for d, t in made),
         in_specs=[vmem] * 4 + [hbm] * 3,
-        out_specs=[vmem] * 3 + [hbm] * 3,
+        out_specs=[vmem] * 6,
         scratch_shapes=[
             pltpu.VMEM(w_gate.shape, BF16),
             pltpu.VMEM(w_up.shape, BF16),
@@ -384,8 +381,6 @@
             pltpu.VMEM((n_dev, PAD, depth), BF16),
             pltpu.VMEM((n_dev, PAD, depth), BF16),
             dma((3,)),
-            dma((items, CORES)),
-            dma((2,)),
             dma,
             dma((GROUPS,)),
             dma((items,)),
@@ -398,44 +393,17 @@
             dma,
         ],
         compiler_params=pltpu.CompilerParams(
-            collective_id=0, has_side_effects=True, vmem_limit_bytes=62 * 1024 * 1024
+            collective_id=0, has_side_effects=True, vmem_limit_bytes=54 * 1024 * 1024
         ),
     )(tokens, cotangent, jnp.transpose(routes), logits, w_gate, w_up, w_down)
-    pair = 2 if chunks % 2 == 0 else 1
-    step = w * pair
-    per = chunks // pair
-
-    def same(i):
-        return (0, 0)
-
-    def whole(a):
-        return pl.BlockSpec(a.shape, same)
-
-    smalls = [whole(small_x), whole(small_r), whole(small_a)]
-    cols = pl.BlockSpec((depth, step), lambda i: (0, i))
     out = pl.pallas_call(
-        weight_kernel,
-        grid=(width // step,),
-        out_shape=(
-            jax.ShapeDtypeStruct(small_x.shape, BF16),
-            jax.ShapeDtypeStruct(small_r.shape, F32),
-            jax.ShapeDtypeStruct(small_a.shape, F32),
-            jax.ShapeDtypeStruct(w_gate.shape, BF16),
-            jax.ShapeDtypeStruct(w_up.shape, BF16),
-            jax.ShapeDtypeStruct(w_down.shape, BF16),
-        ),
-        in_specs=[
-            whole(all_x),
-            whole(all_dy),
-            pl.BlockSpec(
-                (None, pair, 3, rows, w),
-                lambda i: (i // per, lax.rem(i, per), 0, 0, 0),
-            ),
-        ]
-        + smalls,
-        out_specs=smalls + [cols, cols, pl.BlockSpec((step, depth), lambda i: (i, 0))],
-        compiler_params=pltpu.CompilerParams(dimension_semantics=("arbitrary",)),
-    )(all_x, all_dy, all_acts, small_x, small_r, small_a)
+        functools.partial(put_kernel, len(made)),
+        out_shape=tuple(jax.ShapeDtypeStruct(d, t) for d, t in made),
+        in_specs=[vmem] * len(made),
+        out_specs=[hbm] * len(made),
+        scratch_shapes=[dma((PIECES * len(made),))],
+        compiler_params=pltpu.CompilerParams(vmem_limit_bytes=1024 * 1024),
+    )(*held)
     return (out[0], jnp.transpose(out[1])) + tuple(out[2:])
 
 

time: 45.5 us -> 41.9 us (0.921)
  Pallas kernels: 44.6 us -> 41.1 us
    pallas_call x1, Pallas kernels: 5.61 us -> 2.88 us  [body(): pl.pallas_call(functools.partial(put_kernel, len(made)), out_shape=tuple(...]
    pallas_call x1, Pallas kernels: 39 us -> 38.2 us  [body(): pl.pallas_call(functools.partial(kernel, n_fsdp, n_ep, chunks), out_shape...]
where the time goes in v1:
time: 41.9 us; the launch traced here: 41.7 us
  Pallas kernels  41.1 us (98%)
  between operations  0.64 us (2%)
    pallas_call x1, Pallas kernels, body(): pl.pallas_call(functools.partial(kernel, n_fsdp, n_ep, chunks), out_shape...  38.2 us
    pallas_call x1, Pallas kernels, body(): pl.pallas_call(functools.partial(put_kernel, len(made)), out_shape=tuple(...  2.88 us

profile of v1, /device:TPU:0, one launch (start us, length us, event | category | flops | bytes accessed | tf_op | source)
XLA Modules:
  0.0 41.7 jit_solution(2197995990697357546)
XLA Ops:
  0.6 38.2 %shard_map.118 = (bf16[8,2048]{1,0:T(8,128)(2,1)S(1)}, f32[2,8]{1,0:T(2,128)S(1)}, f32[8,8]{1,0:T(8,128)S(1)}, bf16[512,2048]{1,0:T(8,128)(2,1)S(1)}, bf16[512,2...) custom-call(bf16[8,2048]{1,0:T(8,128)(2,1)} %tok_ref.1, bf16[8,2048]{1,0:T(8,128)(2,1)} %cot_ref.1, s32[2,8]{1,0:T(2,128)} %bitcast.2, ...), custom_call_target="tpu_custom_call" | custom-call | tf_op jit(solution)/shard_map/pallas_call | solution.py:359
  38.9 2.9 %shard_map.119 = (bf16[8,2048]{1,0:T(8,128)(2,1)}, f32[2,8]{1,0:T(2,128)}, f32[8,8]{1,0:T(8,128)}, bf16[512,2048]{1,0:T(8,128)(2,1)}, bf16[512,2048]{1,0:T(8,128)(2,1)}, /*index=5*/bf16[2048,512]{1,0:T(8,128)(2,1)}) custom-call(bf16[8,2048]{1,0:T(8,128)(2,1)S(1)} %get-tuple-element.18.refs_0_, f32[2,8]{1,0:T(2,128)S(1)} %get-tuple-element.19.refs_1_, ...), custom_call_target="tpu_custom_call" | custom-call | tf_op jit(solution)/shard_map/pallas_call | solution.py:399

commit v2 on v1

--- a/solution.py
+++ b/solution.py
@@ -12,7 +12,8 @@
 PAD = 8
 CORES = 2
 CHUNKS = 4
-GROUPS = 2
+GROUPS = EXP_WIN
+LANES = 128
 PIECES = 4
 LAST = (((1,), (1,)), ((), ()))
 FIRST = (((0,), (0,)), ((), ()))
@@ -26,13 +27,13 @@
 
 
 def kernel(
-    n_fsdp, n_ep, chunks,
-    tok_ref, cot_ref, routes_ref, logits_ref, wg_hbm, wu_hbm, wd_hbm,
+    n_fsdp, n_ep, chunks, sub,
+    tok_hbm, cot_hbm, routes_hbm, logits_hbm, wg_hbm, wu_hbm, wd_hbm,
     gt_ref, rd_ref, aux_ref, og, ou, od,
-    wg, wu, wd,
+    tok_ref, cot_ref, routes_ref, logits_ref, wg, wu, wd,
     send1, recv1, rows_x, rows_dy,
-    own_a, send_a, recv_a, send_b, recv_b, acts, recv_c, dx, dots, send2, recv2,
-    w_sem, d_send, d_recv, a_send, a_recv, b_send, b_recv, c_send, c_recv, r_send, r_recv,
+    own_a, send_a, recv_a, send_b, recv_b, acts, recv_c, dx, dots, send2, recv2, put, final,
+    i_sem, w_sem, d_send, d_recv, s_send, s_recv, a_send, a_recv, b_send, b_recv, c_send, c_recv, r_send, r_recv,
 ):
     n_dev = n_fsdp * n_ep
     n_x = n_fsdp // CORES
@@ -41,31 +42,45 @@
     me = f * n_ep + e
     x, core = f // CORES, lax.rem(f, CORES)
     partner = x * CORES + (1 - core)
+    half_of, block = e // blocks, lax.rem(e, blocks)
+    other = 1 - half_of
     depth, width = wg.shape
     half = width // CORES
     w = half // chunks
-    ring = n_ep // GROUPS
-    size = n_fsdp * ring
+    size = n_fsdp * blocks
     span_rows = size * CAP
-    place = f * ring + e // GROUPS
-
-    def peer(t, i):
-        return i // ring, lax.rem(i, ring) * GROUPS + lax.rem(e + t, GROUPS)
+    place = block * n_fsdp + f
+    pieces = depth // LANES
+
+    def member(t, i):
+        return lax.rem(i, n_fsdp), (half_of if t == 0 else other) * blocks + i // n_fsdp
 
     barrier = pltpu.get_barrier_semaphore()
 
     def greet(j, _):
-        d = lax.rem(me + j, n_dev)
-        pl.semaphore_signal(barrier, inc=1, device_id=(d // n_ep, lax.rem(d, n_ep)), device_id_type=MESH)
+        pl.semaphore_signal(barrier, inc=1, device_id=member(0, lax.rem(place + j, size)), device_id_type=MESH)
         return 0
 
-    lax.fori_loop(1, n_dev, greet, 0)
+    def greet_other(j, _):
+        pl.semaphore_signal(barrier, inc=1, device_id=(j, other * blocks + block), device_id_type=MESH)
+        return 0
+
+    lax.fori_loop(0, n_fsdp, greet_other, 0)
+    lax.fori_loop(1, size, greet, 0)
+    smalls = [
+        pltpu.make_async_copy(s, t, i_sem.at[i])
+        for i, (s, t) in enumerate(
+            ((routes_hbm, routes_ref), (logits_hbm, logits_ref), (tok_hbm, tok_ref), (cot_hbm, cot_ref))
+        )
+    ]
     loads = [
         pltpu.make_async_copy(s, t, w_sem.at[i])
         for i, (s, t) in enumerate(((wg_hbm, wg), (wu_hbm, wu), (wd_hbm, wd)))
     ]
-    for c in loads:
+    for c in smalls + loads:
         c.start()
+    for c in smalls:
+        c.wait()
 
     routes = routes_ref[...]
     logits = logits_ref[...]
@@ -81,14 +96,9 @@
     e0, e1 = jnp.exp(c0 - top), jnp.exp(c1 - top)
     p0, p1 = e0 / (e0 + e1), e1 / (e0 + e1)
     ci = iota((PAD, n_tok), 0)
-    lanes = iota((n_tok, depth), 1)
-    counts = jnp.sum(
-        jnp.where(lanes == r0, 1.0, 0.0) + jnp.where(lanes == r1, 1.0, 0.0), axis=0, keepdims=True
-    )
     tok = tok_ref[...]
     cot = cot_ref[...].astype(F32)
-    member_col, slot_col, member_row, slot_line = [], [], [], []
-    row_id = iota((PAD, depth), 0)
+    member_col, slot_col = [], []
     for k in range(EXP_WIN):
         m0, m1 = jnp.where(r0 == k, 1.0, 0.0), jnp.where(r1 == k, 1.0, 0.0)
         col = m0 + m1
@@ -97,8 +107,6 @@
         slot_row = jnp.sum(jnp.where(ti < tj, col, 0.0), axis=0, keepdims=True)
         slot_col.append(jnp.sum(jnp.where(tj < ti, row, 0.0), axis=1, keepdims=True))
         member_col.append(col)
-        member_row.append(row)
-        slot_line.append(slot_row)
         cf = ci.astype(F32)
         sel_a = jnp.where((cf == slot_row) & (ci < CAP), row, 0.0).astype(BF16)
         sel_b = jnp.where((cf - CAP == slot_row) & (ci < 2 * CAP), row, 0.0).astype(BF16)
@@ -106,44 +114,91 @@
         sent = jnp.dot(sel_a, tok, preferred_element_type=F32)
         sent = sent + jnp.dot(sel_b, wcot, preferred_element_type=F32)
         for g in range(n_fsdp):
-            part = sent[:, g * depth : (g + 1) * depth]
-            send1[k, g] = jnp.where(row_id == 2 * CAP, counts, part).astype(BF16)
-
-    pl.semaphore_wait(barrier, n_dev - 1)
-
-    recv1[place] = send1[e // blocks, f]
-    for t in range(GROUPS):
-        back_t = (GROUPS - t) % GROUPS
-
-        def push(j, _, t=t, back_t=back_t):
-            df, de = peer(t, lax.rem(place + j, size))
-            pltpu.make_async_remote_copy(
-                src_ref=send1.at[de // blocks, df], dst_ref=recv1.at[back_t * size + place],
-                send_sem=d_send, recv_sem=d_recv.at[back_t], device_id=(df, de), device_id_type=MESH,
-            ).start()
+            send1[k, g] = sent[:, g * depth : (g + 1) * depth].astype(BF16)
+
+    pl.semaphore_wait(barrier, size - 1 + n_fsdp)
+
+    def push(j, _):
+        i = lax.rem(place + j, size)
+        pltpu.make_async_remote_copy(
+            src_ref=send1.at[half_of, lax.rem(i, n_fsdp)], dst_ref=recv1.at[place],
+            send_sem=d_send, recv_sem=d_recv.at[0], device_id=member(0, i), device_id_type=MESH,
+        ).start()
+        return 0
+
+    def push_other(j, _):
+        g = lax.rem(f + j, n_fsdp)
+        pltpu.make_async_remote_copy(
+            src_ref=send1.at[other, g], dst_ref=recv1.at[size + place],
+            send_sem=d_send, recv_sem=d_recv.at[1], device_id=(g, other * blocks + block), device_id_type=MESH,
+        ).start()
+        return 0
+
+    lax.fori_loop(1, size, push, 0)
+    lax.fori_loop(0, n_fsdp, push_other, 0)
+    recv1[place] = send1[half_of, f]
+
+    shared = recv1.at[pl.ds(size + block * n_fsdp, n_fsdp)]
+
+    def share(j):
+        return pltpu.make_async_remote_copy(
+            src_ref=shared, dst_ref=shared, send_sem=s_send, recv_sem=s_recv,
+            device_id=(f, half_of * blocks + lax.rem(block + j, blocks)), device_id_type=MESH,
+        )
+
+    def relay():
+        pltpu.make_async_copy(shared, shared, d_recv.at[1]).wait()
+
+        def one(j, _):
+            share(j).start()
             return 0
 
-        lax.fori_loop(1 if t == 0 else 0, size, push, 0)
+        lax.fori_loop(1, blocks, one, 0)
 
     grp = min(16, size)
+    lanes = iota((n_tok, LANES), 1)
+    counts = jnp.sum(
+        jnp.where(lanes == r0, 1.0, 0.0) + jnp.where(lanes == r1, 1.0, 0.0), axis=0, keepdims=True
+    )
+    raised = jnp.exp(logits - jnp.max(logits, axis=1, keepdims=True))
+    probs = raised / jnp.sum(raised, axis=1, keepdims=True)
+    put_shape = (grp * sub, (pieces + 1) * grp * CAP)
+    pi, pj = iota(put_shape, 0), iota(put_shape, 1)
+    pr = lax.rem(pj, grp * CAP)
+    put[...] = jnp.where(
+        (pi // sub == pr // CAP) & (lax.rem(pi, sub) == pj // (grp * CAP) * CAP + lax.rem(pr, CAP)), 1.0, 0.0
+    ).astype(BF16)
+    reach = n_ep * sub
+    fj = iota((n_tok, reach), 1)
+    fk, fs = fj // (blocks * sub), lax.rem(fj, sub).astype(F32)
+    picks = []
+    for q in range(pieces):
+        row = jnp.zeros((n_tok, reach), F32)
+        for k in range(EXP_WIN):
+            row = row + jnp.where((fk == k) & (fs == slot_col[k] + q * CAP), member_col[k], 0.0)
+        picks.append(row)
+    for k in range(EXP_WIN):
+        picks.append(jnp.where((fk == k) & (fs == slot_col[k] + pieces * CAP), member_col[k], 0.0))
+    picks.append(jnp.where(fs == (pieces + 1) * CAP, 1.0, 0.0))
+    final[...] = jnp.concatenate(picks, axis=0).astype(BF16)
+
     si, sj = iota((grp * CAP, grp * PAD), 0), iota((grp * CAP, grp * PAD), 1)
     base = (si // CAP) * PAD + lax.rem(si, CAP)
     pick_x = jnp.where(sj == base, 1.0, 0.0).astype(BF16)
     pick_dy = jnp.where(sj == base + CAP, 1.0, 0.0).astype(BF16)
-    pick_c = jnp.where(
-        lax.rem(iota((8, grp * PAD), 1), PAD) == 2 * CAP, 1.0, 0.0
-    ).astype(BF16)
-
-    def prepare(t, total):
-        landed = recv1.at[pl.ds(t * size, size - 1 if t == 0 else size)]
-        pltpu.make_async_copy(landed, landed, d_recv.at[t]).wait()
+
+    def prepare(t):
+        if t == 0:
+            landed = recv1.at[pl.ds(0, size - 1)]
+            pltpu.make_async_copy(landed, landed, d_recv.at[0]).wait()
+        elif blocks > 1:
+            landed = recv1.at[pl.ds(0, (blocks - 1) * n_fsdp)]
+            pltpu.make_async_copy(landed, landed, s_recv).wait()
         for g in range(t * size // grp, (t + 1) * size // grp):
             came = recv1[g * grp : (g + 1) * grp].reshape(grp * PAD, depth)
             span = pl.ds(g * grp * CAP, grp * CAP)
             rows_x[span] = jnp.dot(pick_x, came, preferred_element_type=F32).astype(BF16)
             rows_dy[span] = jnp.dot(pick_dy, came, preferred_element_type=F32).astype(BF16)
-            total = total + jnp.dot(pick_c, came, preferred_element_type=F32)
-        return total
 
     def copy_a(k):
         return pltpu.make_async_remote_copy(
@@ -236,40 +291,36 @@
 
     for c in loads:
         c.wait()
-    total = jnp.zeros((8, depth), F32)
     for t in range(GROUPS):
-        total = prepare(t, total)
+        prepare(t)
         for k in range(t * chunks, (t + 1) * chunks):
             stage1(k)
             if k > 0:
                 stage2(k - 1)
+            if k == 1:
+                relay()
+        if chunks == 1 and t == 0:
+            relay()
     stage2(GROUPS * chunks - 1)
 
-    count = total[0:1, 0:n_exp]
-    target = n_exp * (count / jnp.sum(count, axis=1, keepdims=True))
-    raised = jnp.exp(logits - jnp.max(logits, axis=1, keepdims=True))
-    probs = raised / jnp.sum(raised, axis=1, keepdims=True)
-    aux_ref[...] = probs * (target - jnp.sum(probs * target, axis=1, keepdims=True))
-
-    bi, bj = iota((grp * PAD, grp * CAP), 0), iota((grp * PAD, grp * CAP), 1)
-    base = (bj // CAP) * PAD + lax.rem(bj, CAP)
-    put_x = jnp.where(bi == base, 1.0, 0.0).astype(BF16)
-    put_dot = jnp.where(bi == base + CAP, 1.0, 0.0).astype(BF16)
     once = jnp.where(x == 0, 1.0, 0.0)
+    mark = lax.rem(iota((grp * sub, LANES), 0), sub) == (pieces + 1) * CAP
 
     def give_back(t):
         for g in range(t * size // grp, (t + 1) * size // grp):
             span = pl.ds(g * grp * CAP, grp * CAP)
-            mine = jnp.broadcast_to(dots[span] * once, (grp * CAP, depth)).astype(BF16)
-            back = jnp.dot(put_x, dx[span].astype(BF16), preferred_element_type=F32)
-            back = back + jnp.dot(put_dot, mine, preferred_element_type=F32)
-            send2[g * grp : (g + 1) * grp] = back.astype(BF16).reshape(grp, PAD, depth)
+            grads = dx[span].astype(BF16)
+            mine = jnp.broadcast_to(dots[span] * once, (grp * CAP, LANES)).astype(BF16)
+            stack = [grads[:, q * LANES : (q + 1) * LANES] for q in range(pieces)] + [mine]
+            back = jnp.dot(put[...], jnp.concatenate(stack, axis=0), preferred_element_type=F32)
+            back = jnp.where(mark, counts, back).astype(BF16)
+            send2[g * grp : (g + 1) * grp] = back.reshape(grp, sub, LANES)
 
         def give(j, _):
             i = lax.rem(place + j, size)
             pltpu.make_async_remote_copy(
                 src_ref=send2.at[t * size + i], dst_ref=recv2.at[me], send_sem=r_send, recv_sem=r_recv,
-                device_id=peer(t, i), device_id_type=MESH,
+                device_id=member(t, i), device_id_type=MESH,
             ).start()
             return 0
 
@@ -287,31 +338,29 @@
     give_back(GROUPS - 1)
     for c in range(chunks):
         weights(c)
-    everyone = recv1.at[pl.ds(0, n_dev - 1)]
     everyone2 = recv2.at[pl.ds(0, n_dev - 1)]
     pltpu.make_async_copy(everyone2, everyone2, r_recv).wait()
 
-    route = [jnp.zeros((1, 1), F32) for _ in range(EXP_WIN * CAP)]
+    rest = jnp.zeros(((EXP_WIN + 1) * n_tok, LANES), F32)
     for g in range(n_fsdp):
-        grad = jnp.zeros((n_tok, depth), F32)
-        for k in range(EXP_WIN):
-            acc = recv2[g * n_ep + k * blocks].astype(F32)
-            for b in range(1, blocks):
-                acc = acc + recv2[g * n_ep + k * blocks + b].astype(F32)
-            for c in range(CAP):
-                pick = jnp.where(slot_col[k] == c, member_col[k], 0.0)
-                grad = grad + pick * acc[c : c + 1, :]
-                route[k * CAP + c] = route[k * CAP + c] + acc[CAP + c : CAP + c + 1, 0:1]
-        gt_ref[:, g * depth : (g + 1) * depth] = grad.astype(BF16)
-    which = iota((EXP_WIN, n_tok), 0)
-    out = jnp.zeros((EXP_WIN, n_tok), F32)
+        came = recv2[g * n_ep : (g + 1) * n_ep].reshape(reach, LANES)
+        made = jnp.dot(final[...], came, preferred_element_type=F32)
+        for q in range(pieces):
+            at = g * depth + q * LANES
+            gt_ref[:, at : at + LANES] = made[q * n_tok : (q + 1) * n_tok].astype(BF16)
+        rest = rest + made[pieces * n_tok :]
     for k in range(EXP_WIN):
-        for c in range(CAP):
-            pick = jnp.where(slot_line[k] == c, member_row[k], 0.0)
-            out = out + jnp.where(which == k, pick * route[k * CAP + c], 0.0)
-    rd_ref[...] = out
-
+        col = rest[k * n_tok : (k + 1) * n_tok, 0:n_tok]
+        rd_ref[k : k + 1, :] = jnp.sum(jnp.where(ti == tj, col, 0.0), axis=0, keepdims=True)
+    count = rest[EXP_WIN * n_tok : EXP_WIN * n_tok + 1, 0:n_exp]
+    target = n_exp * (count / jnp.sum(count, axis=1, keepdims=True))
+    aux_ref[...] = probs * (target - jnp.sum(probs * target, axis=1, keepdims=True))
+
+    everyone = recv1.at[pl.ds(0, size - 1 + n_fsdp)]
     pltpu.make_async_copy(everyone, everyone, d_send).wait()
+    if blocks > 1:
+        passed = recv1.at[pl.ds(0, (blocks - 1) * n_fsdp)]
+        pltpu.make_async_copy(passed, passed, s_send).wait()
     pltpu.make_async_copy(everyone2, everyone2, r_send).wait()
     for k in range(GROUPS * chunks):
         copy_a(k).wait_send()
@@ -345,6 +394,9 @@
     chunks = max(1, min(CHUNKS, half // 128))
     w = half // chunks
     items, part = GROUPS * chunks, rows // GROUPS
+    pieces = depth // LANES
+    sub = -(-((pieces + 1) * CAP + 1) // 8) * 8
+    grp = min(16, n_dev // EXP_WIN)
     vmem = pl.BlockSpec(memory_space=pltpu.VMEM)
     hbm = pl.BlockSpec(memory_space=pl.ANY)
     dma = pltpu.SemaphoreType.DMA
@@ -357,11 +409,15 @@
         (w_down.shape, BF16),
     )
     held = pl.pallas_call(
-        functools.partial(kernel, n_fsdp, n_ep, chunks),
+        functools.partial(kernel, n_fsdp, n_ep, chunks, sub),
         out_shape=tuple(pltpu.VMEM(d, t) for d, t in made),
-        in_specs=[vmem] * 4 + [hbm] * 3,
+        in_specs=[hbm] * 7,
         out_specs=[vmem] * 6,
         scratch_shapes=[
+            pltpu.VMEM(tokens.shape, BF16),
+            pltpu.VMEM(cotangent.shape, BF16),
+            pltpu.VMEM(routes.shape[::-1], routes.dtype),
+            pltpu.VMEM(logits.shape, F32),
             pltpu.VMEM(w_gate.shape, BF16),
             pltpu.VMEM(w_up.shape, BF16),
             pltpu.VMEM(w_down.shape, BF16),
@@ -378,11 +434,16 @@
             pltpu.VMEM((items, 3, part, w), BF16),
             pltpu.VMEM((rows, depth), F32),
             pltpu.VMEM((rows, 1), F32),
-            pltpu.VMEM((n_dev, PAD, depth), BF16),
-            pltpu.VMEM((n_dev, PAD, depth), BF16),
+            pltpu.VMEM((n_dev, sub, LANES), BF16),
+            pltpu.VMEM((n_dev, sub, LANES), BF16),
+            pltpu.VMEM((grp * sub, (pieces + 1) * grp * CAP), BF16),
+            pltpu.VMEM(((pieces + EXP_WIN + 1) * n_tok, n_ep * sub), BF16),
+            dma((4,)),
             dma((3,)),
             dma,
             dma((GROUPS,)),
+            dma,
+            dma,
             dma((items,)),
             dma((items,)),
             dma((items, n_x - 1)),

time: 41.9 us -> 39.9 us (0.952)
  Pallas kernels: 41.1 us -> 39.1 us
    pallas_call x1, Pallas kernels: 38.2 us -> 36.2 us  [body(): pl.pallas_call(functools.partial(kernel, n_fsdp, n_ep, chunks, sub), out_...]
where the time goes in v2:
time: 39.9 us; the launch traced here: 39.7 us
  Pallas kernels  39.1 us (98%)
  between operations  0.64 us (2%)
    pallas_call x1, Pallas kernels, body(): pl.pallas_call(functools.partial(kernel, n_fsdp, n_ep, chunks, sub), out_...  36.2 us
    pallas_call x1, Pallas kernels, body(): pl.pallas_call(functools.partial(put_kernel, len(made)), out_shape=tuple(...  2.88 us

profile of v2, /device:TPU:0, one launch (start us, length us, event | category | flops | bytes accessed | tf_op | source)
XLA Modules:
  0.0 39.7 jit_solution(10757648523259836170)
XLA Ops:
  0.6 36.2 %shard_map.118 = (bf16[8,2048]{1,0:T(8,128)(2,1)S(1)}, f32[2,8]{1,0:T(2,128)S(1)}, f32[8,8]{1,0:T(8,128)S(1)}, bf16[512,2048]{1,0:T(8,128)(2,1)S(1)}, bf16[512,2...) custom-call(bf16[8,2048]{1,0:T(8,128)(2,1)} %tok_hbm.1, bf16[8,2048]{1,0:T(8,128)(2,1)} %cot_hbm.1, s32[2,8]{1,0:T(2,128)} %bitcast.2, ...), custom_call_target="tpu_custom_call" | custom-call | tf_op jit(solution)/shard_map/pallas_call | solution.py:411
  36.8 2.9 %shard_map.119 = (bf16[8,2048]{1,0:T(8,128)(2,1)}, f32[2,8]{1,0:T(2,128)}, f32[8,8]{1,0:T(8,128)}, bf16[512,2048]{1,0:T(8,128)(2,1)}, bf16[512,2048]{1,0:T(8,128)(2,1)}, /*index=5*/bf16[2048,512]{1,0:T(8,128)(2,1)}) custom-call(bf16[8,2048]{1,0:T(8,128)(2,1)S(1)} %get-tuple-element.18.refs_0_, f32[2,8]{1,0:T(2,128)S(1)} %get-tuple-element.19.refs_1_, ...), custom_call_target="tpu_custom_call" | custom-call | tf_op jit(solution)/shard_map/pallas_call | solution.py:460

commit v3 on v2

--- a/solution.py
+++ b/solution.py
@@ -9,7 +9,6 @@
 
 EXP_WIN = 2
 CAP = 3
-PAD = 8
 CORES = 2
 CHUNKS = 4
 GROUPS = EXP_WIN
@@ -27,12 +26,12 @@
 
 
 def kernel(
-    n_fsdp, n_ep, chunks, sub,
+    n_fsdp, n_ep, chunks, sub, pack,
     tok_hbm, cot_hbm, routes_hbm, logits_hbm, wg_hbm, wu_hbm, wd_hbm,
     gt_ref, rd_ref, aux_ref, og, ou, od,
     tok_ref, cot_ref, routes_ref, logits_ref, wg, wu, wd,
     send1, recv1, rows_x, rows_dy,
-    own_a, send_a, recv_a, send_b, recv_b, acts, recv_c, dx, dots, send2, recv2, put, final,
+    own_a, send_a, recv_a, send_b, recv_b, acts, recv_c, dx, dots, send2, recv2, put, pick, final,
     i_sem, w_sem, d_send, d_recv, s_send, s_recv, a_send, a_recv, b_send, b_recv, c_send, c_recv, r_send, r_recv,
 ):
     n_dev = n_fsdp * n_ep
@@ -52,35 +51,46 @@
     place = block * n_fsdp + f
     pieces = depth // LANES
 
-    def member(t, i):
-        return lax.rem(i, n_fsdp), (half_of if t == 0 else other) * blocks + i // n_fsdp
-
-    barrier = pltpu.get_barrier_semaphore()
-
-    def greet(j, _):
-        pl.semaphore_signal(barrier, inc=1, device_id=member(0, lax.rem(place + j, size)), device_id_type=MESH)
-        return 0
-
-    def greet_other(j, _):
-        pl.semaphore_signal(barrier, inc=1, device_id=(j, other * blocks + block), device_id_type=MESH)
-        return 0
-
-    lax.fori_loop(0, n_fsdp, greet_other, 0)
-    lax.fori_loop(1, size, greet, 0)
+    columns_f = [lax.rem(f + j, n_fsdp) for j in range(n_fsdp)]
+
+    def visit(act, own):
+        def row(j, first=0):
+            b = lax.rem(block + j, blocks)
+            for g in columns_f[first:]:
+                act(g, b)
+
+        if blocks <= 4:
+            for j in range(1, blocks):
+                row(j)
+        else:
+            lax.fori_loop(1, blocks, lambda j, _: (row(j), 0)[1], 0)
+        row(0, 0 if own else 1)
+
     smalls = [
         pltpu.make_async_copy(s, t, i_sem.at[i])
         for i, (s, t) in enumerate(
             ((routes_hbm, routes_ref), (logits_hbm, logits_ref), (tok_hbm, tok_ref), (cot_hbm, cot_ref))
         )
     ]
+    for c in smalls:
+        c.start()
+
+    barrier = pltpu.get_barrier_semaphore()
+
+    def greet(g, at):
+        pl.semaphore_signal(barrier, inc=1, device_id=(g, at), device_id_type=MESH)
+
+    for g in columns_f:
+        greet(g, other * blocks + block)
+    visit(lambda g, b: greet(g, half_of * blocks + b), False)
     loads = [
         pltpu.make_async_copy(s, t, w_sem.at[i])
         for i, (s, t) in enumerate(((wg_hbm, wg), (wu_hbm, wu), (wd_hbm, wd)))
     ]
-    for c in smalls + loads:
-        c.start()
     for c in smalls:
         c.wait()
+    for c in loads:
+        c.start()
 
     routes = routes_ref[...]
     logits = logits_ref[...]
@@ -95,47 +105,57 @@
     top = jnp.maximum(c0, c1)
     e0, e1 = jnp.exp(c0 - top), jnp.exp(c1 - top)
     p0, p1 = e0 / (e0 + e1), e1 / (e0 + e1)
-    ci = iota((PAD, n_tok), 0)
-    tok = tok_ref[...]
-    cot = cot_ref[...].astype(F32)
+    spread = pieces * n_tok
+    wi, wj = iota((pack, 2 * spread), 0), iota((pack, 2 * spread), 1)
+    wq, wp = wi // (2 * CAP), lax.rem(wi, 2 * CAP)
+    want = (wq == lax.rem(wj, spread) // n_tok) & (wp // CAP == wj // spread)
+    slot_of = lax.rem(wp, CAP).astype(F32)
+    ui, uj = iota((n_tok, 2 * spread), 0), lax.rem(iota((n_tok, 2 * spread), 1), n_tok)
+
+    def cut(v):
+        return jnp.concatenate(
+            [
+                jnp.concatenate(
+                    [v[:, g * depth + q * LANES : g * depth + (q + 1) * LANES] for g in range(n_fsdp)], axis=1
+                )
+                for q in range(pieces)
+            ],
+            axis=0,
+        )
+
+    tok = cut(tok_ref[...].astype(F32))
+    cot = cut(cot_ref[...].astype(F32))
     member_col, slot_col = [], []
     for k in range(EXP_WIN):
         m0, m1 = jnp.where(r0 == k, 1.0, 0.0), jnp.where(r1 == k, 1.0, 0.0)
         col = m0 + m1
         weight = m0 * p0 + m1 * p1
+        mine = jnp.sum(jnp.where(ui == uj, col, 0.0), axis=0, keepdims=True)
+        slot = jnp.sum(jnp.where(ui < uj, col, 0.0), axis=0, keepdims=True)
         row = jnp.sum(jnp.where(ti == tj, col, 0.0), axis=0, keepdims=True)
-        slot_row = jnp.sum(jnp.where(ti < tj, col, 0.0), axis=0, keepdims=True)
         slot_col.append(jnp.sum(jnp.where(tj < ti, row, 0.0), axis=1, keepdims=True))
         member_col.append(col)
-        cf = ci.astype(F32)
-        sel_a = jnp.where((cf == slot_row) & (ci < CAP), row, 0.0).astype(BF16)
-        sel_b = jnp.where((cf - CAP == slot_row) & (ci < 2 * CAP), row, 0.0).astype(BF16)
-        wcot = (cot * weight).astype(BF16)
-        sent = jnp.dot(sel_a, tok, preferred_element_type=F32)
-        sent = sent + jnp.dot(sel_b, wcot, preferred_element_type=F32)
+        sel = jnp.where(want & (slot_of == slot), mine, 0.0).astype(BF16)
+        weighted = cot * jnp.concatenate([weight] * pieces, axis=0)
+        both = jnp.concatenate([tok, weighted], axis=0).astype(BF16)
+        sent = jnp.dot(sel, both, preferred_element_type=F32).astype(BF16)
         for g in range(n_fsdp):
-            send1[k, g] = sent[:, g * depth : (g + 1) * depth].astype(BF16)
+            send1[k, g] = sent[:, g * LANES : (g + 1) * LANES]
 
     pl.semaphore_wait(barrier, size - 1 + n_fsdp)
 
-    def push(j, _):
-        i = lax.rem(place + j, size)
+    def push(g, b):
         pltpu.make_async_remote_copy(
-            src_ref=send1.at[half_of, lax.rem(i, n_fsdp)], dst_ref=recv1.at[place],
-            send_sem=d_send, recv_sem=d_recv.at[0], device_id=member(0, i), device_id_type=MESH,
+            src_ref=send1.at[half_of, g], dst_ref=recv1.at[place], send_sem=d_send, recv_sem=d_recv.at[0],
+            device_id=(g, half_of * blocks + b), device_id_type=MESH,
         ).start()
-        return 0
-
-    def push_other(j, _):
-        g = lax.rem(f + j, n_fsdp)
+
+    visit(push, False)
+    for g in columns_f:
         pltpu.make_async_remote_copy(
             src_ref=send1.at[other, g], dst_ref=recv1.at[size + place],
             send_sem=d_send, recv_sem=d_recv.at[1], device_id=(g, other * blocks + block), device_id_type=MESH,
         ).start()
-        return 0
-
-    lax.fori_loop(1, size, push, 0)
-    lax.fori_loop(0, n_fsdp, push_other, 0)
     recv1[place] = send1[half_of, f]
 
     shared = recv1.at[pl.ds(size + block * n_fsdp, n_fsdp)]
@@ -182,10 +202,13 @@
     picks.append(jnp.where(fs == (pieces + 1) * CAP, 1.0, 0.0))
     final[...] = jnp.concatenate(picks, axis=0).astype(BF16)
 
-    si, sj = iota((grp * CAP, grp * PAD), 0), iota((grp * CAP, grp * PAD), 1)
-    base = (si // CAP) * PAD + lax.rem(si, CAP)
-    pick_x = jnp.where(sj == base, 1.0, 0.0).astype(BF16)
-    pick_dy = jnp.where(sj == base + CAP, 1.0, 0.0).astype(BF16)
+    rows = grp * CAP
+    pick_shape = (2 * pieces * rows, grp * pack)
+    si, sj = iota(pick_shape, 0), iota(pick_shape, 1)
+    sr, sb = lax.rem(si, rows), si // rows
+    pick[...] = jnp.where(
+        sj == sr // CAP * pack + lax.rem(sb, pieces) * 2 * CAP + sb // pieces * CAP + lax.rem(sr, CAP), 1.0, 0.0
+    ).astype(BF16)
 
     def prepare(t):
         if t == 0:
@@ -195,10 +218,13 @@
             landed = recv1.at[pl.ds(0, (blocks - 1) * n_fsdp)]
             pltpu.make_async_copy(landed, landed, s_recv).wait()
         for g in range(t * size // grp, (t + 1) * size // grp):
-            came = recv1[g * grp : (g + 1) * grp].reshape(grp * PAD, depth)
-            span = pl.ds(g * grp * CAP, grp * CAP)
-            rows_x[span] = jnp.dot(pick_x, came, preferred_element_type=F32).astype(BF16)
-            rows_dy[span] = jnp.dot(pick_dy, came, preferred_element_type=F32).astype(BF16)
+            came = recv1[g * grp : (g + 1) * grp].reshape(grp * pack, LANES)
+            found = jnp.dot(pick[...], came, preferred_element_type=F32).astype(BF16)
+            span = pl.ds(g * rows, rows)
+            for q in range(pieces):
+                at = slice(q * LANES, (q + 1) * LANES)
+                rows_x[span, at] = found[q * rows : (q + 1) * rows]
+                rows_dy[span, at] = found[(pieces + q) * rows : (pieces + q + 1) * rows]
 
     def copy_a(k):
         return pltpu.make_async_remote_copy(
@@ -291,17 +317,19 @@
 
     for c in loads:
         c.wait()
-    for t in range(GROUPS):
-        prepare(t)
-        for k in range(t * chunks, (t + 1) * chunks):
-            stage1(k)
-            if k > 0:
-                stage2(k - 1)
-            if k == 1:
-                relay()
-        if chunks == 1 and t == 0:
+    lead = max(1, chunks - 1)
+    order = [*range(lead), *range(chunks, 2 * chunks), *range(lead, chunks)]
+    prepare(0)
+    for i, k in enumerate(order):
+        if i == lead:
+            stage2(order[i - 1])
+            prepare(1)
+        stage1(k)
+        if i > 0 and i != lead:
+            stage2(order[i - 1])
+        if i == 0:
             relay()
-    stage2(GROUPS * chunks - 1)
+    stage2(order[-1])
 
     once = jnp.where(x == 0, 1.0, 0.0)
     mark = lax.rem(iota((grp * sub, LANES), 0), sub) == (pieces + 1) * CAP
@@ -316,29 +344,40 @@
             back = jnp.where(mark, counts, back).astype(BF16)
             send2[g * grp : (g + 1) * grp] = back.reshape(grp, sub, LANES)
 
-        def give(j, _):
-            i = lax.rem(place + j, size)
+        def give(g, b):
             pltpu.make_async_remote_copy(
-                src_ref=send2.at[t * size + i], dst_ref=recv2.at[me], send_sem=r_send, recv_sem=r_recv,
-                device_id=member(t, i), device_id_type=MESH,
+                src_ref=send2.at[t * size + b * n_fsdp + g], dst_ref=recv2.at[me], send_sem=r_send, recv_sem=r_recv,
+                device_id=(g, (other if t else half_of) * blocks + b), device_id_type=MESH,
             ).start()
-            return 0
-
-        lax.fori_loop(1 if t == 0 else 0, size, give, 0)
+
+        visit(give, t > 0)
         if t == 0:
             recv2[me] = send2[place]
 
-    for k in range(GROUPS * chunks):
+    for i, k in enumerate(order):
         stage3(k)
-        if k > 0:
-            stage4(k - 1)
-            if k % chunks == 0:
-                give_back(k // chunks - 1)
-    stage4(GROUPS * chunks - 1)
-    give_back(GROUPS - 1)
+        if i > 0 and order[i - 1] != 2 * chunks - 1:
+            stage4(order[i - 1])
+        if k == 2 * chunks - 1:
+            stage4(k)
+            give_back(1)
+    if order[-1] != 2 * chunks - 1:
+        stage4(order[-1])
+    give_back(0)
     for c in range(chunks):
         weights(c)
     everyone2 = recv2.at[pl.ds(0, n_dev - 1)]
+    everyone = recv1.at[pl.ds(0, size - 1 + n_fsdp)]
+    pltpu.make_async_copy(everyone, everyone, d_send).wait()
+    if blocks > 1:
+        passed = recv1.at[pl.ds(0, (blocks - 1) * n_fsdp)]
+        pltpu.make_async_copy(passed, passed, s_send).wait()
+    pltpu.make_async_copy(everyone2, everyone2, r_send).wait()
+    for k in range(GROUPS * chunks):
+        copy_a(k).wait_send()
+        copy_c(k).wait_send()
+        for j in range(1, n_x):
+            copy_b(k, j).wait_send()
     pltpu.make_async_copy(everyone2, everyone2, r_recv).wait()
 
     rest = jnp.zeros(((EXP_WIN + 1) * n_tok, LANES), F32)
@@ -353,20 +392,8 @@
         col = rest[k * n_tok : (k + 1) * n_tok, 0:n_tok]
         rd_ref[k : k + 1, :] = jnp.sum(jnp.where(ti == tj, col, 0.0), axis=0, keepdims=True)
     count = rest[EXP_WIN * n_tok : EXP_WIN * n_tok + 1, 0:n_exp]
-    target = n_exp * (count / jnp.sum(count, axis=1, keepdims=True))
+    target = n_exp * (count / (2 * n_tok * n_dev))
     aux_ref[...] = probs * (target - jnp.sum(probs * target, axis=1, keepdims=True))
-
-    everyone = recv1.at[pl.ds(0, size - 1 + n_fsdp)]
-    pltpu.make_async_copy(everyone, everyone, d_send).wait()
-    if blocks > 1:
-        passed = recv1.at[pl.ds(0, (blocks - 1) * n_fsdp)]
-        pltpu.make_async_copy(passed, passed, s_send).wait()
-    pltpu.make_async_copy(everyone2, everyone2, r_send).wait()
-    for k in range(GROUPS * chunks):
-        copy_a(k).wait_send()
-        copy_c(k).wait_send()
-        for j in range(1, n_x):
-            copy_b(k, j).wait_send()
 
 
 def put_kernel(n, *refs):
@@ -396,6 +423,7 @@
     items, part = GROUPS * chunks, rows // GROUPS
     pieces = depth // LANES
     sub = -(-((pieces + 1) * CAP + 1) // 8) * 8
+    pack = -(-2 * CAP * pieces // 8) * 8
     grp = min(16, n_dev // EXP_WIN)
     vmem = pl.BlockSpec(memory_space=pltpu.VMEM)
     hbm = pl.BlockSpec(memory_space=pl.ANY)
@@ -409,7 +437,7 @@
         (w_down.shape, BF16),
     )
     held = pl.pallas_call(
-        functools.partial(kernel, n_fsdp, n_ep, chunks, sub),
+        functools.partial(kernel, n_fsdp, n_ep, chunks, sub, pack),
         out_shape=tuple(pltpu.VMEM(d, t) for d, t in made),
         in_specs=[hbm] * 7,
         out_specs=[vmem] * 6,
@@ -421,8 +449,8 @@
             pltpu.VMEM(w_gate.shape, BF16),
             pltpu.VMEM(w_up.shape, BF16),
             pltpu.VMEM(w_down.shape, BF16),
-            pltpu.VMEM((EXP_WIN, n_fsdp, PAD, depth), BF16),
-            pltpu.VMEM((n_dev, PAD, depth), BF16),
+            pltpu.VMEM((EXP_WIN, n_fsdp, pack, LANES), BF16),
+            pltpu.VMEM((n_dev, pack, LANES), BF16),
             pltpu.VMEM((rows, depth), BF16),
             pltpu.VMEM((rows, depth), BF16),
             pltpu.VMEM((items, 3, part, w), F32),
@@ -437,6 +465,7 @@
             pltpu.VMEM((n_dev, sub, LANES), BF16),
             pltpu.VMEM((n_dev, sub, LANES), BF16),
             pltpu.VMEM((grp * sub, (pieces + 1) * grp * CAP), BF16),
+            pltpu.VMEM((2 * pieces * grp * CAP, grp * pack), BF16),
             pltpu.VMEM(((pieces + EXP_WIN + 1) * n_tok, n_ep * sub), BF16),
             dma((4,)),
             dma((3,)),

time: 39.9 us -> 36.8 us (0.922)
  Pallas kernels: 39.1 us -> 36 us
    pallas_call x1, Pallas kernels: 36.2 us -> 33.1 us  [body(): pl.pallas_call(functools.partial(kernel, n_fsdp, n_ep, chunks, sub, pack)...]
where the time goes in v3:
time: 36.8 us; the launch traced here: 36.6 us
  Pallas kernels  36 us (98%)
  between operations  0.64 us (2%)
    pallas_call x1, Pallas kernels, body(): pl.pallas_call(functools.partial(kernel, n_fsdp, n_ep, chunks, sub, pack)...  33.1 us
    pallas_call x1, Pallas kernels, body(): pl.pallas_call(functools.partial(put_kernel, len(made)), out_shape=tuple(...  2.88 us

profile of v3, /device:TPU:0, one launch (start us, length us, event | category | flops | bytes accessed | tf_op | source)
XLA Modules:
  0.0 36.6 jit_solution(16717999490524990448)
XLA Ops:
  0.6 33.1 %shard_map.118 = (bf16[8,2048]{1,0:T(8,128)(2,1)S(1)}, f32[2,8]{1,0:T(2,128)S(1)}, f32[8,8]{1,0:T(8,128)S(1)}, bf16[512,2048]{1,0:T(8,128)(2,1)S(1)}, bf16[512,2...) custom-call(bf16[8,2048]{1,0:T(8,128)(2,1)} %tok_hbm.1, bf16[8,2048]{1,0:T(8,128)(2,1)} %cot_hbm.1, s32[2,8]{1,0:T(2,128)} %bitcast.2, ...), custom_call_target="tpu_custom_call" | custom-call | tf_op jit(solution)/shard_map/pallas_call | solution.py:439
  33.7 2.9 %shard_map.119 = (bf16[8,2048]{1,0:T(8,128)(2,1)}, f32[2,8]{1,0:T(2,128)}, f32[8,8]{1,0:T(8,128)}, bf16[512,2048]{1,0:T(8,128)(2,1)}, bf16[512,2048]{1,0:T(8,128)(2,1)}, /*index=5*/bf16[2048,512]{1,0:T(8,128)(2,1)}) custom-call(bf16[8,2048]{1,0:T(8,128)(2,1)S(1)} %get-tuple-element.18.refs_0_, f32[2,8]{1,0:T(2,128)S(1)} %get-tuple-element.19.refs_1_, ...), custom_call_target="tpu_custom_call" | custom-call | tf_op jit(solution)/shard_map/pallas_call | solution.py:489

commit v4 on v3

--- a/solution.py
+++ b/solution.py
@@ -10,10 +10,14 @@
 EXP_WIN = 2
 CAP = 3
 CORES = 2
-CHUNKS = 4
+FRONT = (1, 2, 2)
+MIDDLE = (1, 2, 2, 2, 1)
+BACK = (2, 1)
+EARLY = True
 GROUPS = EXP_WIN
 LANES = 128
-PIECES = 4
+PIECES = 8
+RING = 4
 LAST = (((1,), (1,)), ((), ()))
 FIRST = (((0,), (0,)), ((), ()))
 F32 = jnp.float32
@@ -25,8 +29,18 @@
     return lax.broadcasted_iota(jnp.int32, shape, axis)
 
 
+def plan(half):
+    if half % (8 * LANES):
+        return ((0, 0, half), (1, 0, half))
+    u = half // 8
+    cuts = FRONT + BACK
+    items = [(0, u * sum(cuts[:i]), u * c) for i, c in enumerate(cuts)]
+    far = [(1, u * sum(MIDDLE[:i]), u * c) for i, c in enumerate(MIDDLE)]
+    return (*items[: len(FRONT)], *far, *items[len(FRONT) :])
+
+
 def kernel(
-    n_fsdp, n_ep, chunks, sub, pack,
+    n_fsdp, n_ep, order, sub, pack,
     tok_hbm, cot_hbm, routes_hbm, logits_hbm, wg_hbm, wu_hbm, wd_hbm,
     gt_ref, rd_ref, aux_ref, og, ou, od,
     tok_ref, cot_ref, routes_ref, logits_ref, wg, wu, wd,
@@ -45,7 +59,6 @@
     other = 1 - half_of
     depth, width = wg.shape
     half = width // CORES
-    w = half // chunks
     size = n_fsdp * blocks
     span_rows = size * CAP
     place = block * n_fsdp + f
@@ -169,11 +182,11 @@
     def relay():
         pltpu.make_async_copy(shared, shared, d_recv.at[1]).wait()
 
-        def one(j, _):
-            share(j).start()
-            return 0
-
-        lax.fori_loop(1, blocks, one, 0)
+        if blocks <= 4:
+            for j in range(1, blocks):
+                share(j).start()
+        else:
+            lax.fori_loop(1, blocks, lambda j, _: (share(j).start(), 0)[1], 0)
 
     grp = min(16, size)
     lanes = iota((n_tok, LANES), 1)
@@ -214,6 +227,7 @@
         if t == 0:
             landed = recv1.at[pl.ds(0, size - 1)]
             pltpu.make_async_copy(landed, landed, d_recv.at[0]).wait()
+            relay()
         elif blocks > 1:
             landed = recv1.at[pl.ds(0, (blocks - 1) * n_fsdp)]
             pltpu.make_async_copy(landed, landed, s_recv).wait()
@@ -226,110 +240,124 @@
                 rows_x[span, at] = found[q * rows : (q + 1) * rows]
                 rows_dy[span, at] = found[(pieces + q) * rows : (pieces + q + 1) * rows]
 
-    def copy_a(k):
+    def cell(item):
+        t, start, wide = item
+        return slice(None), pl.ds(t * span_rows, span_rows), pl.ds(start, wide)
+
+    def copy_a(i):
+        at = cell(order[i])
         return pltpu.make_async_remote_copy(
-            src_ref=send_a.at[k], dst_ref=recv_a.at[k], send_sem=a_send.at[k], recv_sem=a_recv.at[k],
+            src_ref=send_a.at[at], dst_ref=recv_a.at[at], send_sem=a_send, recv_sem=a_recv.at[i % RING],
             device_id=(partner, e), device_id_type=MESH,
         )
 
-    def copy_b(k, j):
+    def copy_b(i, j):
+        at = cell(order[i])
         to = lax.rem(x + j, n_x) * CORES + core
         return pltpu.make_async_remote_copy(
-            src_ref=send_b.at[k], dst_ref=recv_b.at[k, j - 1], send_sem=b_send.at[k, j - 1],
-            recv_sem=b_recv.at[k, j - 1], device_id=(to, e), device_id_type=MESH,
+            src_ref=send_b.at[at], dst_ref=recv_b.at[(j - 1, *at)], send_sem=b_send, recv_sem=b_recv.at[i, j - 1],
+            device_id=(to, e), device_id_type=MESH,
         )
 
-    def copy_c(k):
+    def copy_c(i):
+        at = cell(order[i])
         return pltpu.make_async_remote_copy(
-            src_ref=acts.at[k], dst_ref=recv_c.at[k], send_sem=c_send.at[k], recv_sem=c_recv.at[k],
+            src_ref=acts.at[at], dst_ref=recv_c.at[at], send_sem=c_send, recv_sem=c_recv.at[i % RING],
             device_id=(partner, e), device_id_type=MESH,
         )
 
-    def columns(h, k):
-        return pl.ds(pl.multiple_of(h * half + k * w, w), w)
-
-    def group(u):
-        return pl.ds(u // chunks * span_rows, span_rows)
-
-    def partials(h, u):
-        cols = columns(h, u % chunks)
-        xs, dys = rows_x[group(u)], rows_dy[group(u)]
+    def columns(h, start, wide):
+        return pl.ds(pl.multiple_of(h * half + start, LANES), wide)
+
+    def group(t):
+        return pl.ds(t * span_rows, span_rows)
+
+    def partials(h, item):
+        t, start, wide = item
+        cols = columns(h, start, wide)
+        xs, dys = rows_x[group(t)], rows_dy[group(t)]
         yield jnp.dot(xs, wg[:, cols], preferred_element_type=F32)
         yield jnp.dot(xs, wu[:, cols], preferred_element_type=F32)
         yield lax.dot_general(dys, wd[cols, :], LAST, preferred_element_type=F32)
 
-    def stage1(k):
-        for i, v in enumerate(partials(1 - core, k)):
-            send_a[k, i] = v.astype(BF16)
-        copy_a(k).start()
-        for i, v in enumerate(partials(core, k)):
-            own_a[k, i] = v
-
-    def stage2(k):
-        copy_a(k).wait_recv()
-        v = own_a[k] + recv_a[k].astype(F32)
-        own_a[k] = v
-        send_b[k] = v.astype(BF16)
+    def stage1(i):
+        _, rows_at, cols_at = cell(order[i])
+        for n, v in enumerate(partials(1 - core, order[i])):
+            send_a[n, rows_at, cols_at] = v.astype(BF16)
+        copy_a(i).start()
+        for n, v in enumerate(partials(core, order[i])):
+            own_a[n, rows_at, cols_at] = v
+
+    def stage2(i):
+        at = cell(order[i])
+        copy_a(i).wait_recv()
+        v = own_a[at] + recv_a[at].astype(F32)
+        own_a[at] = v
+        send_b[at] = v.astype(BF16)
         for j in range(1, n_x):
-            copy_b(k, j).start()
-
-    def stage3(k):
+            copy_b(i, j).start()
+
+    def stage3(i):
+        t, _, wide = order[i]
+        _, rows_at, cols_at = cell(order[i])
         for j in range(1, n_x):
-            copy_b(k, j).wait_recv()
+            copy_b(i, j).wait_recv()
         pre = []
-        for i in range(3):
-            v = own_a[k, i]
+        for n in range(3):
+            v = own_a[n, rows_at, cols_at]
             for j in range(n_x - 1):
-                v = v + recv_b[k, j, i].astype(F32)
+                v = v + recv_b[j, n, rows_at, cols_at].astype(F32)
             pre.append(v)
         gate_pre, up_pre, hidden_grad = pre
         sigma = jax.nn.sigmoid(gate_pre)
         active = gate_pre * sigma
         hidden = (active * up_pre).astype(BF16)
-        dot = jnp.sum(hidden.astype(F32) * hidden_grad, axis=1, keepdims=True)
-        dots[group(k)] = dot if k % chunks == 0 else dots[group(k)] + dot
-        acts[k, 0] = (hidden_grad * up_pre * sigma * (1.0 + gate_pre * (1.0 - sigma))).astype(BF16)
-        acts[k, 1] = (hidden_grad * active).astype(BF16)
-        acts[k, 2] = hidden
-        copy_c(k).start()
-
-    def grads(h, k, source):
-        cols = columns(h, k % chunks)
-        part = lax.dot_general(source[k, 0], wg[:, cols], LAST, preferred_element_type=F32)
-        return part + lax.dot_general(source[k, 1], wu[:, cols], LAST, preferred_element_type=F32)
-
-    def weights(c):
+        acts[0, rows_at, cols_at] = (
+            hidden_grad * up_pre * sigma * (1.0 + gate_pre * (1.0 - sigma))
+        ).astype(BF16)
+        acts[1, rows_at, cols_at] = (hidden_grad * active).astype(BF16)
+        acts[2, rows_at, cols_at] = hidden
+        copy_c(i).start()
+        prod = hidden.astype(F32) * hidden_grad
+        dot = sum(prod[:, p : p + LANES] for p in range(0, wide, LANES))
+        dots[group(t)] = dot if i == opening[t] else dots[group(t)] + dot
+
+    def grads(h, i, source):
+        _, rows_at, cols_at = cell(order[i])
+        cols = columns(h, *order[i][1:])
+        part = lax.dot_general(source[0, rows_at, cols_at], wg[:, cols], LAST, preferred_element_type=F32)
+        return part + lax.dot_general(source[1, rows_at, cols_at], wu[:, cols], LAST, preferred_element_type=F32)
+
+    def weights(start, wide):
+        at = pl.ds(start, wide)
         for h, source in ((core, acts), (1 - core, recv_c)):
-            cols = columns(h, c)
-            ga, ua, hid = (
-                jnp.concatenate([source[t * chunks + c, i] for t in range(GROUPS)], axis=0) for i in range(3)
-            )
+            cols = columns(h, start, wide)
             xs, dys = rows_x[...], rows_dy[...]
-            og[:, cols] = lax.dot_general(xs, ga, FIRST, preferred_element_type=F32).astype(BF16)
-            ou[:, cols] = lax.dot_general(xs, ua, FIRST, preferred_element_type=F32).astype(BF16)
-            od[cols, :] = lax.dot_general(hid, dys, FIRST, preferred_element_type=F32).astype(BF16)
-
-    def stage4(k):
-        part = grads(core, k, acts)
-        copy_c(k).wait_recv()
-        part = part + grads(1 - core, k, recv_c)
-        dx[group(k)] = part if k % chunks == 0 else dx[group(k)] + part
-
+            og[:, cols] = lax.dot_general(xs, source[0, :, at], FIRST, preferred_element_type=F32).astype(BF16)
+            ou[:, cols] = lax.dot_general(xs, source[1, :, at], FIRST, preferred_element_type=F32).astype(BF16)
+            od[cols, :] = lax.dot_general(source[2, :, at], dys, FIRST, preferred_element_type=F32).astype(BF16)
+
+    def stage4(i):
+        t = order[i][0]
+        part = grads(core, i, acts)
+        copy_c(i).wait_recv()
+        part = part + grads(1 - core, i, recv_c)
+        dx[group(t)] = part if i == opening[t] else dx[group(t)] + part
+
+    opening = [next(i for i, item in enumerate(order) if item[0] == t) for t in range(GROUPS)]
+    closing = [max(i for i, item in enumerate(order) if item[0] == t) for t in range(GROUPS)]
+    n_items = len(order)
     for c in loads:
         c.wait()
-    lead = max(1, chunks - 1)
-    order = [*range(lead), *range(chunks, 2 * chunks), *range(lead, chunks)]
     prepare(0)
-    for i, k in enumerate(order):
-        if i == lead:
-            stage2(order[i - 1])
+    for i in range(n_items):
+        if i == opening[1]:
+            stage2(i - 1)
             prepare(1)
-        stage1(k)
-        if i > 0 and i != lead:
-            stage2(order[i - 1])
-        if i == 0:
-            relay()
-    stage2(order[-1])
+        stage1(i)
+        if i > 0 and i != opening[1]:
+            stage2(i - 1)
+    stage2(n_items - 1)
 
     once = jnp.where(x == 0, 1.0, 0.0)
     mark = lax.rem(iota((grp * sub, LANES), 0), sub) == (pieces + 1) * CAP
@@ -338,7 +366,8 @@
         for g in range(t * size // grp, (t + 1) * size // grp):
             span = pl.ds(g * grp * CAP, grp * CAP)
             grads = dx[span].astype(BF16)
-            mine = jnp.broadcast_to(dots[span] * once, (grp * CAP, LANES)).astype(BF16)
+            mine = jnp.sum(dots[span], axis=1, keepdims=True) * once
+            mine = jnp.broadcast_to(mine, (grp * CAP, LANES)).astype(BF16)
             stack = [grads[:, q * LANES : (q + 1) * LANES] for q in range(pieces)] + [mine]
             back = jnp.dot(put[...], jnp.concatenate(stack, axis=0), preferred_element_type=F32)
             back = jnp.where(mark, counts, back).astype(BF16)
@@ -354,18 +383,22 @@
         if t == 0:
             recv2[me] = send2[place]
 
-    for i, k in enumerate(order):
-        stage3(k)
-        if i > 0 and order[i - 1] != 2 * chunks - 1:
-            stage4(order[i - 1])
-        if k == 2 * chunks - 1:
-            stage4(k)
+    for i in range(n_items):
+        if EARLY and i - 1 == closing[1]:
+            stage4(i - 1)
             give_back(1)
-    if order[-1] != 2 * chunks - 1:
-        stage4(order[-1])
+        stage3(i)
+        if i > 0 and not (EARLY and i - 1 == closing[1]):
+            stage4(i - 1)
+            if i - 1 == closing[1]:
+                give_back(1)
+    stage4(n_items - 1)
+    if closing[1] == n_items - 1:
+        give_back(1)
     give_back(0)
-    for c in range(chunks):
-        weights(c)
+    block_w = min(half, 2 * LANES)
+    for start in range(0, half, block_w):
+        weights(start, block_w)
     everyone2 = recv2.at[pl.ds(0, n_dev - 1)]
     everyone = recv1.at[pl.ds(0, size - 1 + n_fsdp)]
     pltpu.make_async_copy(everyone, everyone, d_send).wait()
@@ -373,11 +406,8 @@
         passed = recv1.at[pl.ds(0, (blocks - 1) * n_fsdp)]
         pltpu.make_async_copy(passed, passed, s_send).wait()
     pltpu.make_async_copy(everyone2, everyone2, r_send).wait()
-    for k in range(GROUPS * chunks):
-        copy_a(k).wait_send()
-        copy_c(k).wait_send()
-        for j in range(1, n_x):
-            copy_b(k, j).wait_send()
+    for buffer, sem in ((send_a, a_send), (recv_b, b_send), (acts, c_send)):
+        pltpu.make_async_copy(buffer, buffer, sem).wait()
     pltpu.make_async_copy(everyone2, everyone2, r_recv).wait()
 
     rest = jnp.zeros(((EXP_WIN + 1) * n_tok, LANES), F32)
@@ -398,17 +428,14 @@
 
 def put_kernel(n, *refs):
     sources, targets, sem = refs[:n], refs[n : 2 * n], refs[2 * n]
-    copies = []
-    for s, t in zip(sources, targets):
+    for i, (s, t) in enumerate(zip(sources, targets)):
         rows = s.shape[0]
         pieces = PIECES if rows % (16 * PIECES) == 0 else 1
         for p in range(pieces):
             span = pl.ds(p * (rows // pieces), rows // pieces)
-            copies.append(pltpu.make_async_copy(s.at[span], t.at[span], sem.at[len(copies)]))
-    for c in copies:
-        c.start()
-    for c in copies:
-        c.wait()
+            pltpu.make_async_copy(s.at[span], t.at[span], sem.at[i]).start()
+    for i, (s, t) in enumerate(zip(sources, targets)):
+        pltpu.make_async_copy(s, t, sem.at[i]).wait()
 
 
 def body(n_fsdp, n_ep, tokens, cotangent, routes, logits, w_gate, w_up, w_down):
@@ -418,9 +445,8 @@
     n_x = n_fsdp // CORES
     rows = n_dev * CAP
     half = width // CORES
-    chunks = max(1, min(CHUNKS, half // 128))
-    w = half // chunks
-    items, part = GROUPS * chunks, rows // GROUPS
+    order = plan(half)
+    items = len(order)
     pieces = depth // LANES
     sub = -(-((pieces + 1) * CAP + 1) // 8) * 8
     pack = -(-2 * CAP * pieces // 8) * 8
@@ -437,7 +463,7 @@
         (w_down.shape, BF16),
     )
     held = pl.pallas_call(
-        functools.partial(kernel, n_fsdp, n_ep, chunks, sub, pack),
+        functools.partial(kernel, n_fsdp, n_ep, order, sub, pack),
         out_shape=tuple(pltpu.VMEM(d, t) for d, t in made),
         in_specs=[hbm] * 7,
         out_specs=[vmem] * 6,
@@ -453,15 +479,15 @@
             pltpu.VMEM((n_dev, pack, LANES), BF16),
             pltpu.VMEM((rows, depth), BF16),
             pltpu.VMEM((rows, depth), BF16),
-            pltpu.VMEM((items, 3, part, w), F32),
-            pltpu.VMEM((items, 3, part, w), BF16),
-            pltpu.VMEM((items, 3, part, w), BF16),
-            pltpu.VMEM((items, 3, part, w), BF16),
-            pltpu.VMEM((items, n_x - 1, 3, part, w), BF16),
-            pltpu.VMEM((items, 3, part, w), BF16),
-            pltpu.VMEM((items, 3, part, w), BF16),
+            pltpu.VMEM((3, rows, half), F32),
+            pltpu.VMEM((3, rows, half), BF16),
+            pltpu.VMEM((3, rows, half), BF16),
+            pltpu.VMEM((3, rows, half), BF16),
+            pltpu.VMEM((n_x - 1, 3, rows, half), BF16),
+            pltpu.VMEM((3, rows, half), BF16),
+            pltpu.VMEM((3, rows, half), BF16),
             pltpu.VMEM((rows, depth), F32),
-            pltpu.VMEM((rows, 1), F32),
+            pltpu.VMEM((rows, LANES), F32),
             pltpu.VMEM((n_dev, sub, LANES), BF16),
             pltpu.VMEM((n_dev, sub, LANES), BF16),
             pltpu.VMEM((grp * sub, (pieces + 1) * grp * CAP), BF16),
@@ -473,12 +499,12 @@
             dma((GROUPS,)),
             dma,
             dma,
-            dma((items,)),
-            dma((items,)),
+            dma,
+            dma((RING,)),
+            dma,
             dma((items, n_x - 1)),
-            dma((items, n_x - 1)),
-            dma((items,)),
-            dma((items,)),
+            dma,
+            dma((RING,)),
             dma,
             dma,
         ],
@@ -491,7 +517,7 @@
         out_shape=tuple(jax.ShapeDtypeStruct(d, t) for d, t in made),
         in_specs=[vmem] * len(made),
         out_specs=[hbm] * len(made),
-        scratch_shapes=[dma((PIECES * len(made),))],
+        scratch_shapes=[dma((len(made),))],
         compiler_params=pltpu.CompilerParams(vmem_limit_bytes=1024 * 1024),
     )(*held)
     return (out[0], jnp.transpose(out[1])) + tuple(out[2:])

time: 36.8 us -> 34.9 us (0.948)
  Pallas kernels: 36 us -> 34 us
    pallas_call x1, Pallas kernels: 33.1 us -> 31.3 us  [body(): pl.pallas_call(functools.partial(kernel, n_fsdp, n_ep, order, sub, pack),...]
where the time goes in v4:
time: 34.9 us; the launch traced here: 34.7 us
  Pallas kernels  34 us (97%)
  between operations  0.64 us (2%)
    pallas_call x1, Pallas kernels, body(): pl.pallas_call(functools.partial(kernel, n_fsdp, n_ep, order, sub, pack),...  31.3 us
    pallas_call x1, Pallas kernels, body(): pl.pallas_call(functools.partial(put_kernel, len(made)), out_shape=tuple(...  2.7 us

profile of v4, /device:TPU:0, one launch (start us, length us, event | category | flops | bytes accessed | tf_op | source)
XLA Modules:
  0.0 34.7 jit_solution(18155844923619265014)
XLA Ops:
  0.6 31.3 %shard_map.118 = (bf16[8,2048]{1,0:T(8,128)(2,1)S(1)}, f32[2,8]{1,0:T(2,128)S(1)}, f32[8,8]{1,0:T(8,128)S(1)}, bf16[512,2048]{1,0:T(8,128)(2,1)S(1)}, bf16[512,2...) custom-call(bf16[8,2048]{1,0:T(8,128)(2,1)} %tok_hbm.1, bf16[8,2048]{1,0:T(8,128)(2,1)} %cot_hbm.1, s32[2,8]{1,0:T(2,128)} %bitcast.2, ...), custom_call_target="tpu_custom_call" | custom-call | tf_op jit(solution)/shard_map/pallas_call | solution.py:465
  32.0 2.7 %shard_map.119 = (bf16[8,2048]{1,0:T(8,128)(2,1)}, f32[2,8]{1,0:T(2,128)}, f32[8,8]{1,0:T(8,128)}, bf16[512,2048]{1,0:T(8,128)(2,1)}, bf16[512,2048]{1,0:T(8,128)(2,1)}, /*index=5*/bf16[2048,512]{1,0:T(8,128)(2,1)}) custom-call(bf16[8,2048]{1,0:T(8,128)(2,1)S(1)} %get-tuple-element.18.refs_0_, f32[2,8]{1,0:T(2,128)S(1)} %get-tuple-element.19.refs_1_, ...), custom_call_target="tpu_custom_call" | custom-call | tf_op jit(solution)/shard_map/pallas_call | solution.py:515

commit v5 on v4

--- a/solution.py
+++ b/solution.py
@@ -79,6 +79,14 @@
             lax.fori_loop(1, blocks, lambda j, _: (row(j), 0)[1], 0)
         row(0, 0 if own else 1)
 
+    barrier = pltpu.get_barrier_semaphore()
+
+    def greet(g, at):
+        pl.semaphore_signal(barrier, inc=1, device_id=(g, at), device_id_type=MESH)
+
+    for g in columns_f:
+        greet(g, other * blocks + block)
+    visit(lambda g, b: greet(g, half_of * blocks + b), False)
     smalls = [
         pltpu.make_async_copy(s, t, i_sem.at[i])
         for i, (s, t) in enumerate(
@@ -88,14 +96,6 @@
     for c in smalls:
         c.start()
 
-    barrier = pltpu.get_barrier_semaphore()
-
-    def greet(g, at):
-        pl.semaphore_signal(barrier, inc=1, device_id=(g, at), device_id_type=MESH)
-
-    for g in columns_f:
-        greet(g, other * blocks + block)
-    visit(lambda g, b: greet(g, half_of * blocks + b), False)
     loads = [
         pltpu.make_async_copy(s, t, w_sem.at[i])
         for i, (s, t) in enumerate(((wg_hbm, wg), (wu_hbm, wu), (wd_hbm, wd)))
@@ -188,7 +188,7 @@
         else:
             lax.fori_loop(1, blocks, lambda j, _: (share(j).start(), 0)[1], 0)
 
-    grp = min(16, size)
+    grp = min(8, size)
     lanes = iota((n_tok, LANES), 1)
     counts = jnp.sum(
         jnp.where(lanes == r0, 1.0, 0.0) + jnp.where(lanes == r1, 1.0, 0.0), axis=0, keepdims=True
@@ -450,7 +450,7 @@
     pieces = depth // LANES
     sub = -(-((pieces + 1) * CAP + 1) // 8) * 8
     pack = -(-2 * CAP * pieces // 8) * 8
-    grp = min(16, n_dev // EXP_WIN)
+    grp = min(8, n_dev // EXP_WIN)
     vmem = pl.BlockSpec(memory_space=pltpu.VMEM)
     hbm = pl.BlockSpec(memory_space=pl.ANY)
     dma = pltpu.SemaphoreType.DMA

time: 34.9 us -> 34.9 us (level)
  no operation moved by 1% of the time
where the time goes in v5:
time: 34.9 us; the launch traced here: 34.7 us
  Pallas kernels  34.1 us (98%)
  between operations  0.64 us (2%)
    pallas_call x1, Pallas kernels, body(): pl.pallas_call(functools.partial(kernel, n_fsdp, n_ep, order, sub, pack),...  31.4 us
    pallas_call x1, Pallas kernels, body(): pl.pallas_call(functools.partial(put_kernel, len(made)), out_shape=tuple(...  2.7 us

profile of v5, /device:TPU:0, one launch (start us, length us, event | category | flops | bytes accessed | tf_op | source)
XLA Modules:
  0.0 34.7 jit_solution(6720296089547022940)
XLA Ops:
  0.6 31.4 %shard_map.118 = (bf16[8,2048]{1,0:T(8,128)(2,1)S(1)}, f32[2,8]{1,0:T(2,128)S(1)}, f32[8,8]{1,0:T(8,128)S(1)}, bf16[512,2048]{1,0:T(8,128)(2,1)S(1)}, bf16[512,2...) custom-call(bf16[8,2048]{1,0:T(8,128)(2,1)} %tok_hbm.1, bf16[8,2048]{1,0:T(8,128)(2,1)} %cot_hbm.1, s32[2,8]{1,0:T(2,128)} %bitcast.2, ...), custom_call_target="tpu_custom_call" | custom-call | tf_op jit(solution)/shard_map/pallas_call | solution.py:465
  32.0 2.7 %shard_map.119 = (bf16[8,2048]{1,0:T(8,128)(2,1)}, f32[2,8]{1,0:T(2,128)}, f32[8,8]{1,0:T(8,128)}, bf16[512,2048]{1,0:T(8,128)(2,1)}, bf16[512,2048]{1,0:T(8,128)(2,1)}, /*index=5*/bf16[2048,512]{1,0:T(8,128)(2,1)}) custom-call(bf16[8,2048]{1,0:T(8,128)(2,1)S(1)} %get-tuple-element.18.refs_0_, f32[2,8]{1,0:T(2,128)S(1)} %get-tuple-element.19.refs_1_, ...), custom_call_target="tpu_custom_call" | custom-call | tf_op jit(solution)/shard_map/pallas_call | solution.py:515
